TPU v7x, 8 devices: a whole 2x2x1 slice. The times are simulated.
8 devices in a mesh: dp: 1 (over z), sz: 2 (over y), sy: 2 (over x), sx: 2 (over core).
Axes of the slice: x: 2, y: 2, z: 1, core: 2. Of those that a mesh axis runs over, the one named last changes fastest.
Arguments:
- rhs_grid: float32 [256, 256, 256], P(('dp', 'sx'), 'sy', 'sz')
- u_start: float32 [256, 256, 256], P(('dp', 'sx'), 'sy', 'sz')
Outputs:
- output: float32 [256, 256, 256], P(('dp', 'sx'), 'sy', 'sz')
All inputs are finite; a program needn't handle non-finite values.
Results may differ from a plain program's by a relative error of at most 0.001.
Values sent between devices are 32-bit elements.
A program may use at most 1 GiB of HBM per device.

v0:
```python
import functools
import jax
import jax.numpy as jnp
from jax import lax
from jax.sharding import PartitionSpec as P

AXIS_NAMES = ('sx', 'sy', 'sz')
LEVELS = 4
SMOOTH_SWEEPS = 2
COARSE_SWEEPS = 16


def send_up(plane, name, count):
    if count == 1:
        return jnp.zeros_like(plane)
    return lax.ppermute(plane, name, [(rank, rank + 1) for rank in range(count - 1)])


def send_down(plane, name, count):
    if count == 1:
        return jnp.zeros_like(plane)
    return lax.ppermute(plane, name, [(rank + 1, rank) for rank in range(count - 1)])


def edge_plane(field, axis, index):
    return lax.slice_in_dim(field, index, index + 1, axis=axis)


def neighbour_sum(field, counts):
    ghosts = []
    for axis in range(3):
        length = field.shape[axis]
        lower = send_up(edge_plane(field, axis, length - 1), AXIS_NAMES[axis], counts[axis])
        upper = send_down(edge_plane(field, axis, 0), AXIS_NAMES[axis], counts[axis])
        ghosts.append((lower, upper))
    total = jnp.zeros_like(field)
    for axis in range(3):
        length = field.shape[axis]
        lower, upper = ghosts[axis]
        total = total + jnp.concatenate([lower, lax.slice_in_dim(field, 0, length - 1, axis=axis)], axis=axis)
        total = total + jnp.concatenate([lax.slice_in_dim(field, 1, length, axis=axis), upper], axis=axis)
    return total


def residual(source, field, stiffness, counts):
    return source - stiffness * (6.0 * field - neighbour_sum(field, counts))


def jacobi_sweep(source, field, stiffness, counts):
    return field + residual(source, field, stiffness, counts) / (9.0 * stiffness)


def restrict_axis(fine, lower, axis):
    half = fine.shape[axis] // 2
    pairs = fine.reshape(fine.shape[:axis] + (half, 2) + fine.shape[axis + 1:])
    even = lax.index_in_dim(pairs, 0, axis + 1, keepdims=False)
    odd = lax.index_in_dim(pairs, 1, axis + 1, keepdims=False)
    odd_prev = jnp.concatenate([lower, lax.slice_in_dim(odd, 0, half - 1, axis=axis)], axis=axis)
    return 0.25 * (odd_prev + odd) + 0.5 * even


def prolong_axis(coarse, upper, axis):
    length = coarse.shape[axis]
    shifted = jnp.concatenate([lax.slice_in_dim(coarse, 1, length, axis=axis), upper], axis=axis)
    stacked = jnp.stack([coarse, 0.5 * (coarse + shifted)], axis=axis + 1)
    return stacked.reshape(coarse.shape[:axis] + (2 * length,) + coarse.shape[axis + 1:])


def restrict(fine, counts):
    for axis in range(3):
        lower = send_up(edge_plane(fine, axis, fine.shape[axis] - 1), AXIS_NAMES[axis], counts[axis])
        fine = restrict_axis(fine, lower, axis)
    return fine


def prolong(coarse, counts):
    for axis in range(3):
        upper = send_down(edge_plane(coarse, axis, 0), AXIS_NAMES[axis], counts[axis])
        coarse = prolong_axis(coarse, upper, axis)
    return coarse


def vcycle(level, source, field, counts, size):
    stiffness = ((size + 1) / 2 ** level) ** 2
    coarsest = level == LEVELS - 1
    sweeps = COARSE_SWEEPS if coarsest else SMOOTH_SWEEPS
    if field is None:
        field = source / (9.0 * stiffness)
        sweeps = sweeps - 1
    for sweep in range(sweeps):
        field = jacobi_sweep(source, field, stiffness, counts)
    if coarsest:
        return field
    coarse_source = restrict(residual(source, field, stiffness, counts), counts)
    correction = vcycle(level + 1, coarse_source, None, counts, size)
    field = field + prolong(correction, counts)
    for sweep in range(SMOOTH_SWEEPS):
        field = jacobi_sweep(source, field, stiffness, counts)
    return field


def solution(mesh):
    counts = (mesh.shape['sx'], mesh.shape['sy'], mesh.shape['sz'])
    spec = P(('dp', 'sx'), 'sy', 'sz')

    def run(rhs_grid, u_start):
        size = rhs_grid.shape[1]
        local_cycle = functools.partial(vcycle, 0, counts=counts, size=size)
        return jax.shard_map(local_cycle, mesh=mesh, in_specs=(spec, spec), out_specs=spec, check_vma=False)(rhs_grid, u_start)
    return run
```

profile of v0, /device:TPU:0, one launch (start us, length us, event | category | flops | bytes accessed | tf_op | source)
XLA Modules:
  0.0 1358.1 jit_solution(16161592767504294811)
XLA Ops:
  0.0 13.4 fusion.517
  38.8 13.3 fusion.516
  52.2 13.2 fusion.518
  82.8 27.4 %fusion.8 = f32[128,128,128]{2,1,0:T(8,128)S(1)} fusion(f32[128,128,128]{2,1,0:T(8,128)} %param.3, f32[128,128,128]{2,1,0:T(8,128)} %param.2, f32[127,128,128]{2,1,0:T(8,128)} %get-tuple-element.88, f32[1,128,128]{2,1,0:T(8,128)S(1)} %collective-permute-done, f32[1,128,128]{2,1,0:T(8,128)S(1)} %collective-permute-done.1, ...), kind=kLoop, calls=%fused_computation.9 | loop fusion | flops 35651584 | bytes 75497472 | tf_op jit(solution)/shard_map/add | solution.py:50
  110.2 8.1 fusion.511
  159.1 10.8 fusion.514
  179.4 27.4 %fusion.17 = f32[128,128,128]{2,1,0:T(8,128)S(1)} fusion(f32[128,128,128]{2,1,0:T(8,128)} %copy-done.3, f32[128,128,128]{2,1,0:T(8,128)} %param.2, f32[127,128,128]{2,1,0:T(8,128)} %get-tuple-element.76, f32[1,128,128]{2,1,0:T(8,128)S(1)} %collective-permute-done.6, f32[1,128,128]{2,1,0:T(8,128)S(1)} %collective-permute-done.7, ...), kind=kLoop, calls=%fused_computation.19 | loop fusion | flops 35651584 | bytes 75497472 | tf_op jit(solution)/shard_map/add | solution.py:50
  206.8 8.1 fusion.505
  255.7 10.8 fusion.508
  275.9 27.3 %fusion.24 = f32[128,128,128]{2,1,0:T(8,128)S(1)} fusion(f32[128,128,128]{2,1,0:T(8,128)} %param.2, f32[127,128,128]{2,1,0:T(8,128)} %get-tuple-element.64, f32[1,128,128]{2,1,0:T(8,128)S(1)} %collective-permute-done.12, f32[1,128,128]{2,1,0:T(8,128)S(1)} %collective-permute-done.13, f32[127,128,128]{2,1,0:T(8,128)} %get-tuple-element.63, ...), kind=kLoop, calls=%fused_computation.27 | loop fusion | flops 31457280 | bytes 75497472 | tf_op jit(solution)/shard_map/sub | solution.py:46
  306.5 8.8 slice_bitcast_fusion.2
  444.2 9.2 fusion.73
  510.4 14.0 %fusion.54 = f32[32,2,64,64]{3,2,0,1:T(8,128)S(1)} fusion(f32[32,2,1,64]{3,2,0,1:T(1,128)S(1)} %copy.5253, f32[32,2,1,64]{3,2,0,1:T(1,128)S(1)} %copy.5257, f32[32,2,64,1]{3,2,0,1:T(8,128)} %copy.5258, f32[32,2,64,1]{3,2,0,1:T(8,128)} %copy.5261, f32[32,2,1,64]{3,2,0,1:T(1,128)S(1)} %copy.5262, f32[32,2,1,64]{3,2,0,1:T(1,128)S(1)} %copy.5266, ...), kind=kLoop, calls=%fused_computation.75 | loop fusion | flops 7602176 | bytes 14680064 | tf_op jit(solution)/shard_map/sub | solution.py:46
  597.0 9.1 collective-permute-done.46
  1009.3 8.4 fusion.101
  1076.1 20.9 %fusion.120 = (f32[64,1,64,64]{3,2,0,1:T(8,128)S(1)}, f32[64,1,64,64]{3,2,0,1:T(8,128)S(1)}) fusion(f32[1,1,64,64]{3,2,0,1:T(8,128)S(1)} %bitcast.992, f32[63,1,64,64]{3,2,0,1:T(8,128)} %slice_bitcast_fusion.6, f32[64,1,64,1]{3,2,0,1:T(8,128)} %copy.5484, f32[64,1,64,63]{3,2,0,1:T(8,128)} %get-tuple-element.133, f32[64,1,64,63]{3,2,0,1:T(8,128)} %get-tuple-element.132, ...), kind=kLoop, calls=%fused_computation.163 | loop fusion | flops 15728640 | bytes 26214400 | tf_op jit(solution)/shard_map/mul | solution.py:65
  1130.4 9.2 copy.5498
  1139.6 9.3 copy.5499
  1148.9 11.9 add.2862
  1160.8 13.4 fusion.499
  1210.1 10.8 fusion.502
  1230.3 27.4 %fusion.33 = f32[128,128,128]{2,1,0:T(8,128)S(1)} fusion(f32[128,128,128]{2,1,0:T(8,128)} %add.2862, f32[128,128,128]{2,1,0:T(8,128)} %param.2, f32[127,128,128]{2,1,0:T(8,128)} %get-tuple-element.46, f32[1,128,128]{2,1,0:T(8,128)S(1)} %collective-permute-done.174, f32[1,128,128]{2,1,0:T(8,128)S(1)} %collective-permute-done.175, ...), kind=kLoop, calls=%fused_computation.39 | loop fusion | flops 35651584 | bytes 75497472 | tf_op jit(solution)/shard_map/add | solution.py:50
  1306.7 10.8 fusion.496
  1326.9 30.9 %fusion.42 = f32[128,128,128]{2,1,0:T(8,128)} fusion(f32[128,128,128]{2,1,0:T(8,128)} %copy-done.2, f32[128,128,128]{2,1,0:T(8,128)} %param.2, f32[127,128,128]{2,1,0:T(8,128)} %get-tuple-element.34, f32[1,128,128]{2,1,0:T(8,128)S(1)} %collective-permute-done.180, f32[1,128,128]{2,1,0:T(8,128)S(1)} %collective-permute-done.181, ...), kind=kLoop, calls=%fused_computation.49 | loop fusion | flops 35651584 | bytes 75497472 | tf_op jit(solution)/shard_map/add | solution.py:50
  (827 shorter events, 999.6 us)
Async XLA Ops:
  18.6 46.8 %collective-permute-start.4 = (f32[128,128,1]{1,0,2:T(8,128)S(1)}, f32[128,128,1]{1,0,2:T(8,128)S(1)}, u32[]{:S(2)}, u32[]{:S(2)}) collective-permute-start(f32[128,128,1]{1,0,2:T(8,128)S(1)} %copy.5529), channel_id=1, source_target_pairs={{0,4},{1,5},{2,6},{3,7}} | collective-permute-start | bytes 196616 | tf_op jit(solution)/shard_map/ppermute | solution.py:16
  29.1 48.9 %collective-permute-start.5 = (f32[128,128,1]{1,0,2:T(8,128)S(1)}, f32[128,128,1]{1,0,2:T(8,128)S(1)}, u32[]{:S(2)}, u32[]{:S(2)}) collective-permute-start(f32[128,128,1]{1,0,2:T(8,128)S(1)} %copy.5530), channel_id=1, source_target_pairs={{4,0},{5,1},{6,2},{7,3}} | collective-permute-start | bytes 196616 | tf_op jit(solution)/shard_map/ppermute | solution.py:22
  31.3 51.5 %collective-permute-start = (f32[1,128,128]{2,1,0:T(8,128)S(1)}, f32[1,128,128]{2,1,0:T(8,128)S(1)}, u32[]{:S(2)}, u32[]{:S(2)}) collective-permute-start(f32[1,128,128]{2,1,0:T(8,128)S(1)} %get-tuple-element.90), channel_id=1, source_target_pairs={{0,1},{2,3},{4,5},{6,7}} | collective-permute-start | bytes 196616 | tf_op jit(solution)/shard_map/ppermute | solution.py:16
  32.8 50.0 %collective-permute-start.1 = (f32[1,128,128]{2,1,0:T(8,128)S(1)}, f32[1,128,128]{2,1,0:T(8,128)S(1)}, u32[]{:S(2)}, u32[]{:S(2)}) collective-permute-start(f32[1,128,128]{2,1,0:T(8,128)S(1)} %get-tuple-element.89), channel_id=1, source_target_pairs={{1,0},{3,2},{5,4},{7,6}} | collective-permute-start | bytes 196616 | tf_op jit(solution)/shard_map/ppermute | solution.py:22
  35.4 47.4 %collective-permute-start.2 = (f32[128,1,128]{2,1,0:T(1,128)S(1)}, f32[128,1,128]{2,1,0:T(1,128)S(1)}, u32[]{:S(2)}, u32[]{:S(2)}) collective-permute-start(f32[128,1,128]{2,1,0:T(1,128)S(1)} %get-tuple-element.86), channel_id=1, source_target_pairs={{0,2},{1,3},{4,6},{5,7}} | collective-permute-start | bytes 196616 | tf_op jit(solution)/shard_map/ppermute | solution.py:16
  148.3 26.5 %collective-permute-start.11 = (f32[128,128,1]{1,0,2:T(8,128)S(1)}, f32[128,128,1]{1,0,2:T(8,128)S(1)}, u32[]{:S(2)}, u32[]{:S(2)}) collective-permute-start(f32[128,128,1]{1,0,2:T(8,128)S(1)} %copy.5204), channel_id=1, source_target_pairs={{4,0},{5,1},{6,2},{7,3}} | collective-permute-start | bytes 196616 | tf_op jit(solution)/shard_map/ppermute | solution.py:22
  149.6 29.8 %collective-permute-start.6 = (f32[1,128,128]{2,1,0:T(8,128)S(1)}, f32[1,128,128]{2,1,0:T(8,128)S(1)}, u32[]{:S(2)}, u32[]{:S(2)}) collective-permute-start(f32[1,128,128]{2,1,0:T(8,128)S(1)} %get-tuple-element.78), channel_id=1, source_target_pairs={{0,1},{2,3},{4,5},{6,7}} | collective-permute-start | bytes 196616 | tf_op jit(solution)/shard_map/ppermute | solution.py:16
  152.0 27.3 %collective-permute-start.7 = (f32[1,128,128]{2,1,0:T(8,128)S(1)}, f32[1,128,128]{2,1,0:T(8,128)S(1)}, u32[]{:S(2)}, u32[]{:S(2)}) collective-permute-start(f32[1,128,128]{2,1,0:T(8,128)S(1)} %get-tuple-element.77), channel_id=1, source_target_pairs={{1,0},{3,2},{5,4},{7,6}} | collective-permute-start | bytes 196616 | tf_op jit(solution)/shard_map/ppermute | solution.py:22
  153.3 26.0 %collective-permute-start.8 = (f32[128,1,128]{2,1,0:T(1,128)S(1)}, f32[128,1,128]{2,1,0:T(1,128)S(1)}, u32[]{:S(2)}, u32[]{:S(2)}) collective-permute-start(f32[128,1,128]{2,1,0:T(1,128)S(1)} %get-tuple-element.74), channel_id=1, source_target_pairs={{0,2},{1,3},{4,6},{5,7}} | collective-permute-start | bytes 196616 | tf_op jit(solution)/shard_map/ppermute | solution.py:16
  244.7 26.5 %collective-permute-start.17 = (f32[128,128,1]{1,0,2:T(8,128)S(1)}, f32[128,128,1]{1,0,2:T(8,128)S(1)}, u32[]{:S(2)}, u32[]{:S(2)}) collective-permute-start(f32[128,128,1]{1,0,2:T(8,128)S(1)} %copy.5208), channel_id=1, source_target_pairs={{4,0},{5,1},{6,2},{7,3}} | collective-permute-start | bytes 196616 | tf_op jit(solution)/shard_map/ppermute | solution.py:22
  246.0 29.8 %collective-permute-start.12 = (f32[1,128,128]{2,1,0:T(8,128)S(1)}, f32[1,128,128]{2,1,0:T(8,128)S(1)}, u32[]{:S(2)}, u32[]{:S(2)}) collective-permute-start(f32[1,128,128]{2,1,0:T(8,128)S(1)} %get-tuple-element.66), channel_id=1, source_target_pairs={{0,1},{2,3},{4,5},{6,7}} | collective-permute-start | bytes 196616 | tf_op jit(solution)/shard_map/ppermute | solution.py:16
  248.5 27.4 %collective-permute-start.13 = (f32[1,128,128]{2,1,0:T(8,128)S(1)}, f32[1,128,128]{2,1,0:T(8,128)S(1)}, u32[]{:S(2)}, u32[]{:S(2)}) collective-permute-start(f32[1,128,128]{2,1,0:T(8,128)S(1)} %get-tuple-element.65), channel_id=1, source_target_pairs={{1,0},{3,2},{5,4},{7,6}} | collective-permute-start | bytes 196616 | tf_op jit(solution)/shard_map/ppermute | solution.py:22
  249.8 26.1 %collective-permute-start.14 = (f32[128,1,128]{2,1,0:T(1,128)S(1)}, f32[128,1,128]{2,1,0:T(1,128)S(1)}, u32[]{:S(2)}, u32[]{:S(2)}) collective-permute-start(f32[128,1,128]{2,1,0:T(1,128)S(1)} %get-tuple-element.62), channel_id=1, source_target_pairs={{0,2},{1,3},{4,6},{5,7}} | collective-permute-start | bytes 196616 | tf_op jit(solution)/shard_map/ppermute | solution.py:16
  330.4 45.2 %collective-permute-start.19 = (f32[64,1,128]{2,1,0:T(1,128)S(1)}, f32[64,1,128]{2,1,0:T(1,128)S(1)}, u32[]{:S(2)}, u32[]{:S(2)}) collective-permute-start(f32[64,1,128]{2,1,0:T(1,128)S(1)} %slice_add_fusion.6), channel_id=1, source_target_pairs={{0,2},{1,3},{4,6},{5,7}} | collective-permute-start | bytes 98312 | tf_op jit(solution)/shard_map/ppermute | solution.py:16
  461.3 29.7 %collective-permute-start.29 = (f32[64,1,64]{2,0,1:T(8,128)S(1)}, f32[64,1,64]{2,0,1:T(8,128)S(1)}, u32[]{:S(2)}, u32[]{:S(2)}) collective-permute-start(f32[64,1,64]{2,0,1:T(8,128)S(1)} %bitcast.1063), channel_id=1, source_target_pairs={{0,2},{1,3},{4,6},{5,7}} | collective-permute-start | bytes 49160 | tf_op jit(solution)/shard_map/ppermute | solution.py:16
  465.8 26.4 %collective-permute-start.27 = (f32[1,64,64]{2,1,0:T(8,128)S(1)}, f32[1,64,64]{2,1,0:T(8,128)S(1)}, u32[]{:S(2)}, u32[]{:S(2)}) collective-permute-start(f32[1,64,64]{2,1,0:T(8,128)S(1)} %get-tuple-element.154), channel_id=1, source_target_pairs={{0,1},{2,3},{4,5},{6,7}} | collective-permute-start | bytes 49160 | tf_op jit(solution)/shard_map/ppermute | solution.py:16
  468.5 23.7 %collective-permute-start.28 = (f32[1,64,64]{2,1,0:T(8,128)S(1)}, f32[1,64,64]{2,1,0:T(8,128)S(1)}, u32[]{:S(2)}, u32[]{:S(2)}) collective-permute-start(f32[1,64,64]{2,1,0:T(8,128)S(1)} %get-tuple-element.155), channel_id=1, source_target_pairs={{1,0},{3,2},{5,4},{7,6}} | collective-permute-start | bytes 49160 | tf_op jit(solution)/shard_map/ppermute | solution.py:22
  474.6 23.6 %collective-permute-start.31 = (f32[64,64,1]{1,0,2:T(8,128)S(1)}, f32[64,64,1]{1,0,2:T(8,128)S(1)}, u32[]{:S(2)}, u32[]{:S(2)}) collective-permute-start(f32[64,64,1]{1,0,2:T(8,128)S(1)} %copy.5245), channel_id=1, source_target_pairs={{0,4},{1,5},{2,6},{3,7}} | collective-permute-start | bytes 49160 | tf_op jit(solution)/shard_map/ppermute | solution.py:16
  1204.2 26.1 %collective-permute-start.174 = (f32[1,128,128]{2,1,0:T(8,128)S(1)}, f32[1,128,128]{2,1,0:T(8,128)S(1)}, u32[]{:S(2)}, u32[]{:S(2)}) collective-permute-start(f32[1,128,128]{2,1,0:T(8,128)S(1)} %get-tuple-element.48), channel_id=1, source_target_pairs={{0,1},{2,3},{4,5},{6,7}} | collective-permute-start | bytes 196616 | tf_op jit(solution)/shard_map/ppermute | solution.py:16
  1205.6 24.6 %collective-permute-start.175 = (f32[1,128,128]{2,1,0:T(8,128)S(1)}, f32[1,128,128]{2,1,0:T(8,128)S(1)}, u32[]{:S(2)}, u32[]{:S(2)}) collective-permute-start(f32[1,128,128]{2,1,0:T(8,128)S(1)} %get-tuple-element.47), channel_id=1, source_target_pairs={{1,0},{3,2},{5,4},{7,6}} | collective-permute-start | bytes 196616 | tf_op jit(solution)/shard_map/ppermute | solution.py:22
  1295.6 26.6 %collective-permute-start.185 = (f32[128,128,1]{1,0,2:T(8,128)S(1)}, f32[128,128,1]{1,0,2:T(8,128)S(1)}, u32[]{:S(2)}, u32[]{:S(2)}) collective-permute-start(f32[128,128,1]{1,0,2:T(8,128)S(1)} %copy.5506), channel_id=1, source_target_pairs={{4,0},{5,1},{6,2},{7,3}} | collective-permute-start | bytes 196616 | tf_op jit(solution)/shard_map/ppermute | solution.py:22
  1296.9 29.9 %collective-permute-start.180 = (f32[1,128,128]{2,1,0:T(8,128)S(1)}, f32[1,128,128]{2,1,0:T(8,128)S(1)}, u32[]{:S(2)}, u32[]{:S(2)}) collective-permute-start(f32[1,128,128]{2,1,0:T(8,128)S(1)} %get-tuple-element.36), channel_id=1, source_target_pairs={{0,1},{2,3},{4,5},{6,7}} | collective-permute-start | bytes 196616 | tf_op jit(solution)/shard_map/ppermute | solution.py:16
  1299.5 27.4 %collective-permute-start.181 = (f32[1,128,128]{2,1,0:T(8,128)S(1)}, f32[1,128,128]{2,1,0:T(8,128)S(1)}, u32[]{:S(2)}, u32[]{:S(2)}) collective-permute-start(f32[1,128,128]{2,1,0:T(8,128)S(1)} %get-tuple-element.35), channel_id=1, source_target_pairs={{1,0},{3,2},{5,4},{7,6}} | collective-permute-start | bytes 196616 | tf_op jit(solution)/shard_map/ppermute | solution.py:22
  1300.8 26.1 %collective-permute-start.182 = (f32[128,1,128]{2,1,0:T(1,128)S(1)}, f32[128,1,128]{2,1,0:T(1,128)S(1)}, u32[]{:S(2)}, u32[]{:S(2)}) collective-permute-start(f32[128,1,128]{2,1,0:T(1,128)S(1)} %get-tuple-element.32), channel_id=1, source_target_pairs={{0,2},{1,3},{4,6},{5,7}} | collective-permute-start | bytes 196616 | tf_op jit(solution)/shard_map/ppermute | solution.py:16
  (216 other events, 2165.2 us)
where the time goes:
time: 1370 us; the launch traced here: 1360 us
  local copies, waits for them, and re-layouts  549 us (40%)
  starting transfers between devices  379 us (28%)
  other arithmetic  299 us (22%)
  waiting for transfers between devices  126 us (9%)
    ppermute x93, starting transfers between devices, send_up(): lax.ppermute(plane, name, [(rank, rank + 1) for rank in range(count - 1)])  256 us
    add x25, other arithmetic, jacobi_sweep(): field + residual(source, field, stiffness, counts) / (9.0 * stiffness)  145 us
    slice x19, local copies, waits for them, and re-layouts, neighbour_sum(): lax.slice_in_dim(field, 1, length, axis=axis)  138 us
    slice x111, local copies, waits for them, and re-layouts, edge_plane(): return lax.slice_in_dim(field, index, index + 1, axis=axis)  136 us
    ppermute x93, starting transfers between devices, send_down(): lax.ppermute(plane, name, [(rank + 1, rank) for rank in range(count - 1)])  123 us
    ppermute x93, waiting for transfers between devices, send_down(): lax.ppermute(plane, name, [(rank + 1, rank) for rank in range(count - 1)])  100 us
    concatenate x70, local copies, waits for them, and re-layouts, neighbour_sum(): jnp.concatenate([lower, lax.slice_in_dim(field, 0, length - 1, axis=axis)...  58.1 us
    sub x5, other arithmetic, residual(): return source - stiffness * (6.0 * field - neighbour_sum(field, counts))  43.6 us
  transfers between devices with their start and end apart: 186, of which 37 were waited for; matrix products, arithmetic and copies ran while one was open for 25% of the time, Pallas kernels for 0%

commit v1 on v0

v1 whole, which is shorter than its diff:
```python
import functools
import jax
import jax.numpy as jnp
from jax import lax
from jax.experimental import pallas as pl
from jax.experimental.pallas import tpu as pltpu
from jax.sharding import PartitionSpec as P

N = 128
PR = 144
NC = 4
CR = 128 // NC
YR = 136
XR = 72
GI = 16
S, W = 8, 128
LAST = W - 1
MESH = pl.DeviceIdType.MESH
F32 = jnp.float32
HI = lax.Precision.HIGHEST


class Lev:
    def __init__(self, n, h, pj, kp, hb, ni, region, unroll, group):
        self.n, self.h, self.pj, self.kp, self.hb, self.ni = n, h, pj, kp, hb, ni
        self.region, self.unroll, self.group = region, unroll, group
        self.nk = n + 2 * kp
        self.planes = n + 2 * pj
        self.rows = self.planes * self.nk


L1 = Lev(64, 4, 6, 8, 8, 128, 68, 4, 1)
L2 = Lev(32, 5, 10, 8, 8, 64, 40, 8, 12)
L3 = Lev(16, 16, 18, 16, 16, 32, 32, 8, 10)
LEVS = (L1, L2, L3)


def up8(x):
    return (x + 7) // 8 * 8


def eight(r):
    return pl.ds(r, S)


def body(h2, f_hbm, u_hbm, out_hbm, A, B, F, Y, X, XP, RXP, TS, KS, PK, RZ, PY, RY,
         G1, V1, W1, G2, V2, W2, G3, V3, W3, E, T2,
         RY1, SZ1, RZ1, RY2, SZ2, RZ2, RY3, SZ3, RZ3,
         ld, st, xs, xr, zs, zr, ys, yr, cs, cr):
    cx, cy, cz = lax.axis_index('sx'), lax.axis_index('sy'), lax.axis_index('sz')
    lane = lax.broadcasted_iota(jnp.int32, (CR, W), 1)
    lane0, lane127 = lane == 0, lane == LAST
    even = lane % 2 == 0
    ninth = F32(1.0 / 9.0)
    px, py, pz = {'sx': 1 - cx}, {'sy': 1 - cy}, {'sz': 1 - cz}
    edge = LAST * (1 - cz)
    bufs = (A, B)

    def flat(ref):
        return ref.reshape(ref.shape[0] * ref.shape[1], ref.shape[2])

    A2, B2, Y2, X2 = flat(A), flat(B), flat(Y), flat(X)
    flats = (A2, B2)

    def chunk_of(c):
        return c * cy + (NC - 1 - c) * (1 - cy)

    def load(k):
        rows = pl.ds(k * CR, CR)
        a = pltpu.make_async_copy(u_hbm.at[:, rows, :], A.at[pl.ds(1, N), pl.ds(S + k * CR, CR), :], ld.at[0, k])
        b = pltpu.make_async_copy(f_hbm.at[:, rows, :], F.at[:, rows, :], ld.at[1, k])
        return a, b
    for k in range(NC):
        for cp in load(k):
            cp.start()

    barrier = pltpu.get_barrier_semaphore()
    for p in (px, py, pz):
        pl.semaphore_signal(barrier, inc=1, device_id=p, device_id_type=MESH)
    pl.semaphore_wait(barrier, 3)

    zero = jnp.zeros((S, W), F32)
    blank = jnp.zeros((CR, W), F32)

    def zero_rows(ref2, count):
        @pl.loop(0, count // 64)
        def _(t):
            ref2[pl.ds(pl.multiple_of(t * 64, 64), 64), :] = jnp.zeros((64, W), F32)
        if count % 64:
            ref2[pl.ds(count // 64 * 64, count % 64), :] = jnp.zeros((count % 64, W), F32)
    for ref in (G1, V1, W1, G2, V2, W2, G3, V3, W3, E):
        zero_rows(ref, ref.shape[0])

    for buf in bufs:
        gx = 129 * cx
        @pl.loop(0, PR // S)
        def _(t):
            buf[gx, eight(pl.multiple_of(t * S, S)), :] = zero

        @pl.loop(0, 130)
        def _(i):
            buf[i, eight(0), :] = zero
            buf[i, eight(136), :] = zero

    @pl.loop(0, 65)
    def _(i):
        Y[i, eight(0), :] = zero

    @pl.loop(0, XR // S)
    def _(t):
        X[W, eight(pl.multiple_of(t * S, S)), :] = zero
    for q in range(5):
        TS[q, eight(0), :] = zero

    def x_copy(par, k):
        rows = pl.ds(pl.multiple_of(S + k * CR, S), CR)
        return pltpu.make_async_remote_copy(
            src_ref=bufs[par].at[W - LAST * cx, rows, :], dst_ref=bufs[par].at[129 * cx, rows, :],
            send_sem=xs.at[par, k], recv_sem=xr.at[par, k], device_id=px, device_id_type=MESH)

    def z_copy(par, k):
        rows = pl.ds(pl.multiple_of(k * CR, S), CR)
        return pltpu.make_async_remote_copy(
            src_ref=PK.at[par, rows, :], dst_ref=RZ.at[par, rows, :],
            send_sem=zs.at[par, k], recv_sem=zr.at[par, k], device_id=pz, device_id_type=MESH)

    def y_copy(par):
        return pltpu.make_async_remote_copy(
            src_ref=PY.at[par], dst_ref=RY.at[par],
            send_sem=ys.at[par], recv_sem=yr.at[par], device_id=py, device_id_type=MESH)

    def send(par, c, k):
        x_copy(par, k).start()
        z_copy(par, k).start()

        @pl.when(c == 0)
        def _():
            j = LAST * (1 - cy)
            for t in range(16):
                PY[par, eight(t * S), :] = flats[par][pl.ds((t * S + 1) * PR + S + j, S, stride=PR), :]
            y_copy(par).start()

    def receive(par, c, k):
        x_copy(par, k).wait()
        z_copy(par, k).wait()

        @pl.when(c == 0)
        def _():
            y_copy(par).wait()
            j = 136 * (1 - cy) + 7 * cy
            for t in range(16):
                flats[par][pl.ds((t * S + 1) * PR + j, S, stride=PR), :] = RY[par, eight(t * S), :]

    def spin(value, i):
        return pltpu.roll(value, (i - edge + 2 * W) & LAST, 1)

    def chunk(k, shift=0):
        return pl.ds(k * CR + shift, CR)

    def pack_group(buf, k, i0, count, first, cols):
        rows = chunk(k, S)
        for q in range(count):
            cols = jnp.where(lane == first + q, spin(buf[i0 + q + 1, rows, :], first + q), cols)
        return cols

    def pack_chunk(par, k):
        def step(t, cols):
            i0 = t * 2 * GI
            return pack_group(bufs[par], k, i0, 2 * GI, i0, cols)
        PK[par, chunk(k), :] = lax.fori_loop(0, N // (2 * GI), step, blank)

    def stencil_chunk(src, par, k, dst, visit, extra):
        ghost = RZ[par, chunk(k), :]
        ghosts = (jnp.where(even, ghost, 0.0), jnp.where(even, 0.0, ghost))
        rows, below, above = chunk(k, S), chunk(k, S - 1), chunk(k, S + 1)

        def side_sums(i0):
            for q in range(GI):
                c = src[i0 + q + 1, rows, :]
                g = pltpu.roll(ghosts[q & 1], (edge - i0 - q + W) & LAST, 1)
                KS[pl.ds(q * CR, CR), :] = jnp.where(lane0, g, pltpu.roll(c, 1, 1)) + jnp.where(
                    lane127, g, pltpu.roll(c, LAST, 1))

        def step(t, state):
            um, uc, cols, extra = state
            i0 = t * GI
            if dst is not None:
                cols = pack_group(dst, k, (i0 + N - GI) % N, GI, i0 - GI, cols)
            for q in range(GI):
                un = src[i0 + q + 2, rows, :]
                total = (um + un) + (src[i0 + q + 1, below, :] + src[i0 + q + 1, above, :]) + KS[pl.ds(q * CR, CR), :]
                extra = visit(t, i0, q, uc, total, extra)
                um, uc = uc, un
            side_sums((i0 + GI) % N)
            return um, uc, cols, extra
        side_sums(0)
        state = (src[0, rows, :], src[1, rows, :], blank, extra)
        _, _, cols, extra = lax.fori_loop(0, N // GI, step, state)
        if dst is not None:
            cols = pack_group(dst, k, N - GI, GI, N - GI, cols)
        return cols, extra

    def sweep_pass(par, first, last):
        src, dst = bufs[par], bufs[1 - par]

        @pl.loop(0, NC)
        def _(c):
            k = chunk_of(c)
            receive(par, c, k)

            def visit(t, i0, q, centre, total, extra):
                fs = F[i0 + q, chunk(k), :]
                if first:
                    fs = fs * F32(h2)
                    F[i0 + q, chunk(k), :] = fs
                dst[i0 + q + 1, chunk(k, S), :] = (3.0 * centre + (total + fs)) * ninth
                return extra
            cols, _ = stencil_chunk(src, par, k, None if last else dst, visit, ())
            if last:
                store(k).start()
            else:
                PK[1 - par, chunk(k), :] = cols
                send(1 - par, c, k)

    def store(k):
        return pltpu.make_async_copy(
            B.at[pl.ds(1, N), pl.ds(pl.multiple_of(S + k * CR, S), CR), :],
            out_hbm.at[:, pl.ds(pl.multiple_of(k * CR, S), CR), :], st.at[k])

    for k in range(NC):
        for cp in load(k):
            cp.wait()

    @pl.loop(0, NC)
    def _(c):
        k = chunk_of(c)
        pack_chunk(0, k)
        send(0, c, k)

    sweep_pass(0, True, False)
    sweep_pass(1, False, False)

    @pl.loop(0, NC)
    def _(c):
        k = chunk_of(c)
        receive(0, c, k)

        def visit(t, i0, q, centre, total, carry):
            low, mid = carry
            r = F[i0 + q, chunk(k), :] - 6.0 * centre + total
            if q % 2 == 0:
                return low, r
            Y[t * (GI // 2) + q // 2, chunk(k, S), :] = (low + r) + 2.0 * mid
            return r, mid
        _, lows = stencil_chunk(A, 0, k, None, visit, (blank, blank))
        Y[64, chunk(k, S), :] = lows[0]

    def restrict_j(src_plane, dst, dst_plane):
        base = src_plane * YR
        lo, mid, hi = (Y2[pl.ds(base + S + d, 64, stride=2), :] for d in (-1, 0, 1))
        dst[pl.ds(pl.multiple_of(dst_plane * XR, S), 64), :] = (lo + hi) + 2.0 * mid
        row = lax.broadcasted_iota(jnp.int32, (S, W), 0)
        dst[eight(pl.multiple_of(dst_plane * XR + 64, S)), :] = jnp.where(
            row == 0, pltpu.roll(Y2[eight(base + W), :], 1, 0), 0.0)

    @pl.loop(0, 64)
    def _(i):
        restrict_j(i, X2, i + 64 * cx)
    restrict_j(64, XP, 0)

    own = pl.ds(64 * cx, 64)
    cpx = [pltpu.make_async_remote_copy(src_ref=X.at[own], dst_ref=X.at[own], send_sem=cs.at[0], recv_sem=cr.at[0],
                                        device_id=px, device_id_type=MESH),
           pltpu.make_async_remote_copy(src_ref=XP, dst_ref=RXP, send_sem=cs.at[1], recv_sem=cr.at[1],
                                        device_id=px, device_id_type=MESH)]
    for cp in cpx:
        cp.start()
    for cp in cpx:
        cp.wait()
    for t in range(9):
        r = eight(t * S)
        X2[eight(64 * XR + t * S), :] += jnp.where(cx == 0, XP[r, :], RXP[r, :])

    @pl.loop(0, 13)
    def _(jo):
      for q in range(5):
        jc = jo * 5 + q
        TS[q, pl.ds(S, W), :] = jnp.transpose(X2[pl.ds(jc, W, stride=XR), :])
        base = (jc + L1.pj) * L1.nk + L1.kp
        lo, mid, hi = (TS[q, pl.ds(S + d, 64, stride=2), :] for d in (-1, 0, 1))
        G1[pl.ds(pl.multiple_of(base, S), 64), :] = ((lo + hi) + 2.0 * mid) * F32(1 / 16)
        G1[pl.ds(base + 64, 1), :] = TS[q, pl.ds(135, 1), :] * F32(1 / 16)

    def wide_exchange(L, G, RYl, SZl, RZl, s):
        cnt = L.h + 1
        js = (L.n - L.h) * (1 - cy)
        cp = pltpu.make_async_remote_copy(
            src_ref=G.at[pl.ds(pl.multiple_of((js + L.pj) * L.nk, S), cnt * L.nk), :], dst_ref=RYl,
            send_sem=cs.at[s], recv_sem=cr.at[s], device_id=py, device_id_type=MESH)
        cp.start()
        cp.wait()
        jd = (L.n * (1 - cy) - L.h * cy + L.pj) * L.nk

        @pl.loop(0, cnt)
        def _(p):
            r = pl.multiple_of(p * L.nk, S)
            G[pl.ds(pl.multiple_of(jd + r, S), L.nk), :] += RYl[pl.ds(r, L.nk), :]
        ks = (L.n - L.h) * (1 - cz) + L.kp
        kd = L.n * (1 - cz) - L.h * cz + L.kp
        jl = L.pj - L.h * cy

        @pl.loop(0, L.n + L.h)
        def _(p):
            SZl[pl.ds(p * cnt, cnt), :] = G[pl.ds((jl + p) * L.nk + ks, cnt), :]
        cp = pltpu.make_async_remote_copy(src_ref=SZl, dst_ref=RZl, send_sem=cs.at[s + 1], recv_sem=cr.at[s + 1],
                                          device_id=pz, device_id_type=MESH)
        cp.start()
        cp.wait()

        @pl.loop(0, L.n + L.h)
        def _(p):
            G[pl.ds((jl + p) * L.nk + kd, cnt), :] += RZl[pl.ds(p * cnt, cnt), :]
            G[pl.ds((jl + p) * L.nk + L.kp - 1 + (L.n + 1) * cz, 1), :] = zero[:1]
        G[pl.ds(pl.multiple_of((L.pj - 1 + (L.n + 1) * cy) * L.nk, S), L.nk), :] = jnp.zeros((L.nk, W), F32)

    def coarse_sum(L, src, r, count):
        lanes = lax.broadcasted_iota(jnp.int32, (count, W), 1)
        c = src[pl.ds(r, count), :]
        left = jnp.where(lanes == 0, 0.0, pltpu.roll(c, 1, 1))
        right = jnp.where(lanes == L.ni - 1, 0.0, pltpu.roll(c, LAST, 1))
        total = (src[pl.ds(r - L.nk, count), :] + src[pl.ds(r + L.nk, count), :]) + (
            src[pl.ds(r - 1, count), :] + src[pl.ds(r + 1, count), :]) + (left + right)
        return c, total

    def coarse_pass(L, src, visit):
        j0 = L.pj - (L.region - L.n) * cy
        k0 = L.kp - L.hb * cz
        count = L.n + L.hb

        @pl.loop(0, L.region // L.unroll)
        def _(po):
            for p in range(L.unroll):
                r = pl.multiple_of((j0 + po * L.unroll + p) * L.nk + k0, S)
                visit(pl.ds(r, count), *coarse_sum(L, src, r, count))

    def first_two(L, G, V):
        def visit(rows, c, total):
            V[rows, :] = (12.0 * c + total) * F32(1 / 81)
        coarse_pass(L, G, visit)

    def smooth(L, G, V, W_):
        def visit(rows, c, total):
            W_[rows, :] = (3.0 * c + (total + G[rows, :])) * ninth
        coarse_pass(L, V, visit)

    def weights(ni, up):
        a = lax.broadcasted_iota(jnp.int32, (W, W), 0)
        b = lax.broadcasted_iota(jnp.int32, (W, W), 1)
        if up:
            fine, coarse = b, a
            w = jnp.where(fine == 2 * coarse, 1.0, 0.0) + jnp.where(
                (fine == 2 * coarse + 1) | (fine == 2 * coarse - 1), 0.5, 0.0)
        else:
            fine, coarse = a, b
            w = jnp.where(fine == 2 * coarse, 2.0, 0.0) + jnp.where(
                (fine == 2 * coarse + 1) | (fine == 2 * coarse - 1), 1.0, 0.0)
        return jnp.where((coarse < ni) & (fine < 2 * ni), w, 0.0).astype(F32)

    def restrict_coarse(L, M, G, V, W_, Gc):
        @pl.loop(0, L.n // 4)
        def _(po):
            for p in range(4):
                r = pl.multiple_of((L.pj + po * 4 + p) * L.nk + L.kp, S)
                c, total = coarse_sum(L, V, r, L.n)
                W_[pl.ds(r, L.n), :] = G[pl.ds(r, L.n), :] - 6.0 * c + total
        for side in (L.pj - 1, L.pj + L.n, L.pj + L.n + 1):
            W_[pl.ds(side * L.nk, L.nk), :] = jnp.zeros((L.nk, W), F32)

        @pl.loop(0, L.n)
        def _(p):
            base = (L.pj + p) * L.nk + L.kp
            W_[eight(pl.multiple_of(base - S, S)), :] = zero
            W_[eight(pl.multiple_of(base + L.n, S)), :] = zero
        w = weights(M.ni, False)

        @pl.loop(0, M.n + 1)
        def _(p):
            base = (L.pj + 2 * p) * L.nk + L.kp
            rows = M.n + 4
            sums = []
            for dj in (-1, 0, 1):
                lo, mid, hi = (W_[pl.ds(base + dj * L.nk + d, rows, stride=2), :] for d in (-1, 0, 1))
                sums.append((lo + hi) + 2.0 * mid)
            T2[pl.ds(p * (M.n + S), rows), :] = (sums[0] + sums[2]) + 2.0 * sums[1]
        hr = M.n + S
        group = (M.n + 1) // (1 + 2 * (M.n // 32))

        @pl.loop(0, (M.n + 1) // group)
        def _(g):
            t0 = pl.multiple_of(g * group * hr, S)
            res = jnp.dot(T2[pl.ds(t0, group * hr), :], w, precision=HI, preferred_element_type=F32) * F32(1 / 16)
            for p in range(group):
                rb = (M.pj + g * group + p) * M.nk + M.kp
                Gc[pl.ds(pl.multiple_of(rb, S), M.n), :] = res[p * hr:p * hr + M.n]
                Gc[pl.ds(rb + M.n, 1), :] = res[p * hr + M.n:p * hr + M.n + 1]

    def prolong_coarse(L, M, V, e):
        w = weights(M.ni, True)
        extra = 3
        j0 = M.pj - extra * cy

        @pl.loop(0, (M.n + extra + 1) // M.group)
        def _(g):
            rows = pl.ds(pl.multiple_of((j0 + g * M.group) * M.nk, S), M.group * M.nk)
            E[rows, :] = jnp.dot(e[rows, :], w, precision=HI, preferred_element_type=F32)

        @pl.loop(0, M.n + extra)
        def _(p):
            jc = j0 + p - M.pj
            fb = (L.pj + 2 * jc) * L.nk + L.kp
            eb = (j0 + p) * M.nk + M.kp
            for kc, rows in ((0, M.n), (M.n * (1 - cz) - 4 * cz, 4)):
                a, b = E[pl.ds(eb + kc, rows), :], E[pl.ds(eb + kc + 1, rows), :]
                c, d = E[pl.ds(eb + M.nk + kc, rows), :], E[pl.ds(eb + M.nk + kc + 1, rows), :]
                ab = a + b
                f = fb + 2 * kc
                V[pl.ds(f, rows, stride=2), :] += a
                V[pl.ds(f + 1, rows, stride=2), :] += 0.5 * ab
                V[pl.ds(f + L.nk, rows, stride=2), :] += 0.5 * (a + c)
                V[pl.ds(f + L.nk + 1, rows, stride=2), :] += 0.25 * (ab + (c + d))

    wide_exchange(L1, G1, RY1, SZ1, RZ1, 2)
    first_two(L1, G1, V1)
    restrict_coarse(L1, L2, G1, V1, W1, G2)
    wide_exchange(L2, G2, RY2, SZ2, RZ2, 4)
    first_two(L2, G2, V2)
    restrict_coarse(L2, L3, G2, V2, W2, G3)
    wide_exchange(L3, G3, RY3, SZ3, RZ3, 6)
    first_two(L3, G3, V3)

    @pl.loop(0, 7)
    def _(s):
        smooth(L3, G3, V3, W3)
        smooth(L3, G3, W3, V3)
    prolong_coarse(L2, L3, V2, V3)
    smooth(L2, G2, V2, W2)
    smooth(L2, G2, W2, V2)
    prolong_coarse(L1, L2, V1, V2)
    smooth(L1, G1, V1, W1)
    smooth(L1, G1, W1, V1)

    @pl.loop(0, 13)
    def _(jo):
      for q in range(5):
        jc = jo * 5 + q
        base = (jc + L1.pj) * L1.nk + L1.kp
        a, b = V1[pl.ds(pl.multiple_of(base, S), 64), :], V1[pl.ds(base + 1, 64), :]
        TS[q, pl.ds(S, 64, stride=2), :] = a
        TS[q, pl.ds(S + 1, 64, stride=2), :] = 0.5 * (a + b)
        X2[pl.ds(jc, W, stride=XR), :] = jnp.transpose(TS[q, pl.ds(S, W), :])

    @pl.loop(0, NC)
    def _(c):
        k = chunk_of(c)

        @pl.loop(0, 64)
        def _(i):
            half = CR // 2
            xb = (i + 64 * cx) * XR + k * half
            a, b = X2[pl.ds(xb, half), :], X2[pl.ds(xb + 1, half), :]
            cc, d = X2[pl.ds(xb + XR, half), :], X2[pl.ds(xb + XR + 1, half), :]
            ab = a + b
            f = (2 * i + 1) * PR + S + k * CR
            for shift, value in ((0, a), (1, 0.5 * ab), (PR, 0.5 * (a + cc)), (PR + 1, 0.25 * (ab + (cc + d)))):
                rows = pl.ds(f + shift, half, stride=2)
                B2[rows, :] = A2[rows, :] + value
        pack_chunk(1, k)
        send(1, c, k)

    sweep_pass(1, False, False)
    sweep_pass(0, False, True)
    for k in range(NC):
        store(k).wait()


def solution(mesh):
    spec = P(('dp', 'sx'), 'sy', 'sz')

    def local(f, u):
        size = 2 * f.shape[1]
        h2 = 1.0 / float((size + 1) ** 2)
        vm = lambda *s: pltpu.VMEM(s, F32)
        scratch = [vm(130, PR, W), vm(130, PR, W), vm(N, N, W), vm(65, YR, W), vm(129, XR, W),
                   vm(XR, W), vm(XR, W), vm(5, 136, W), vm(GI * CR, W), vm(2, N, W), vm(2, N, W), vm(2, N, W), vm(2, N, W)]
        for L in LEVS:
            scratch += [vm(L.rows, W)] * 3
        scratch += [vm(max(L2.rows, L3.rows), W), vm(33 * 40, W)]
        for L in LEVS:
            z = up8((L.n + L.h) * (L.h + 1))
            scratch += [vm((L.h + 1) * L.nk, W), vm(z, W), vm(z, W)]
        dma = pltpu.SemaphoreType.DMA
        scratch += [dma((2, NC)), dma((NC,)), dma((2, NC)), dma((2, NC)), dma((2, NC)), dma((2, NC)), dma((2,)), dma((2,)),
                    dma((S,)), dma((S,))]
        return pl.pallas_call(
            functools.partial(body, h2),
            out_shape=jax.ShapeDtypeStruct(f.shape, F32),
            in_specs=[pl.BlockSpec(memory_space=pl.ANY)] * 2,
            out_specs=pl.BlockSpec(memory_space=pl.ANY),
            scratch_shapes=scratch,
            compiler_params=pltpu.CompilerParams(collective_id=0, has_side_effects=True, vmem_limit_bytes=67043328),
        )(f, u)

    def run(rhs_grid, u_start):
        return jax.shard_map(local, mesh=mesh, in_specs=(spec, spec), out_specs=spec, check_vma=False)(rhs_grid, u_start)
    return run
```

time: 1370 us -> 163 us (0.12)
  local copies, waits for them, and re-layouts: 549 us -> 7.89 us
  starting transfers between devices: 379 us -> 0 us
  other arithmetic: 299 us -> 0 us
  Pallas kernels: 0 us -> 155 us
  waiting for transfers between devices: 126 us -> 0 us
    ppermute x186 -> x0, starting transfers between devices: 379 us -> none  [the longest x93 256 us: send_up(): lax.ppermute(plane, name, [(rank, rank + 1) for rank in range(count - 1)])]
    slice x144 -> x0, local copies, waits for them, and re-layouts: 303 us -> none  [the longest x19 138 us: neighbour_sum(): lax.slice_in_dim(field, 1, length, axis=axis)]
    add x42 -> x0, other arithmetic: 188 us -> none  [the longest x25 145 us: jacobi_sweep(): field + residual(source, field, stiffness, counts) / (9.0 * stiffness)]
    pallas_call x0 -> x1, Pallas kernels: none -> 155 us  [local(): pl.pallas_call(functools.partial(body, h2), out_shape=jax.ShapeDtypeStruc...]
    ppermute x186 -> x0, waiting for transfers between devices: 126 us -> none  [the longest x93 100 us: send_down(): lax.ppermute(plane, name, [(rank + 1, rank) for rank in range(count - 1)])]
    concatenate x101 -> x0, local copies, waits for them, and re-layouts: 93 us -> none  [the longest x70 58.1 us: neighbour_sum(): jnp.concatenate([lower, lax.slice_in_dim(field, 0, length - 1, axis=axis)...]
    ppermute x22 -> x0, local copies, waits for them, and re-layouts: 66.9 us -> none  [the longest x13 35.5 us: send_up(): lax.ppermute(plane, name, [(rank, rank + 1) for rank in range(count - 1)])]
    sub x5 -> x0, other arithmetic: 43.6 us -> none  [residual(): return source - stiffness * (6.0 * field - neighbour_sum(field, counts))]
  transfers between devices with their start and end apart: 186 -> 0, of which waited for: 37 -> 0; matrix products, arithmetic and copies ran while one was open for 25% -> 0% of each run, Pallas kernels for 0% -> 0%
where the time goes in v1:
time: 163 us
  Pallas kernels  155 us (95%)
  local copies, waits for them, and re-layouts  7.89 us (5%)
    pallas_call x1, Pallas kernels, local(): pl.pallas_call(functools.partial(body, h2), out_shape=jax.ShapeDtypeStruc...  155 us
    unnamed x1, local copies, waits for them, and re-layouts  7.89 us

profile of v1, /device:TPU:0, one launch (start us, length us, event | category | flops | bytes accessed | tf_op | source)
XLA Modules:
  0.0 162.7 jit_solution(1119509455885007113)
XLA Ops:
  0.0 154.8 %shard_map.28 = f32[128,128,128]{2,1,0:T(8,128)} custom-call(f32[128,128,128]{2,1,0:T(8,128)} %f_hbm.1, f32[128,128,128]{2,1,0:T(8,128)} %u_hbm.1), custom_call_target="tpu_custom_call" | custom-call | tf_op jit(solution)/shard_map/pallas_call | solution.py:504
  154.8 7.9 %copy.4 = f32[128,128,128]{2,1,0:T(8,128)} copy(f32[128,128,128]{2,1,0:T(8,128)} %shard_map.28) | data formatting | bytes 16777216

commit v2 on v1

v2 whole, which is shorter than its diff:
```python
import functools
import jax
import jax.numpy as jnp
from jax import lax
from jax.experimental import pallas as pl
from jax.experimental.pallas import tpu as pltpu
from jax.sharding import PartitionSpec as P

N = 128
PR = 144
NC = 4
XR = 72
CP = N // NC
GP = 4
GC = CP // GP
NG = N // GP
RB = 32
S, W = 8, 128
LAST = W - 1
MESH = pl.DeviceIdType.MESH
F32 = jnp.float32
HI = lax.Precision.HIGHEST


class Lev:
    def __init__(self, n, h, pj, kp, hb, ni, region, unroll, group):
        self.n, self.h, self.pj, self.kp, self.hb, self.ni = n, h, pj, kp, hb, ni
        self.region, self.unroll, self.group = region, unroll, group
        self.nk = n + 2 * kp
        self.planes = n + 2 * pj
        self.rows = self.planes * self.nk


L1 = Lev(64, 4, 6, 8, 8, 128, 68, 4, 1)
L2 = Lev(32, 5, 10, 8, 8, 64, 40, 8, 12)
L3 = Lev(16, 16, 18, 16, 16, 32, 32, 8, 10)
LEVS = (L1, L2, L3)


def up8(x):
    return (x + 7) // 8 * 8


def eight(r):
    return pl.ds(r, S)


def body(h2, f_hbm, u_hbm, out_hbm, A, B, AT, BT, F, X, XP, RXP, TS, KS, PZ, RZ, PY, RY,
         G2, V2, W2, G3, V3, W3, E, T2,
         RY1, SZ1, RZ1, RY2, SZ2, RZ2, RY3, SZ3, RZ3,
         ld, st, xs, xr, zs, zr, ys, yr, cs, cr):
    cx, cy, cz = lax.axis_index('sx'), lax.axis_index('sy'), lax.axis_index('sz')
    ninth = F32(1.0 / 9.0)
    px, py, pz = {'sx': 1 - cx}, {'sy': 1 - cy}, {'sz': 1 - cz}
    bufs = (A, B)

    def flat(ref):
        return ref.reshape(ref.shape[0] * ref.shape[1], ref.shape[2])

    A2, B2, X2 = flat(A), flat(B), flat(X)
    flats, turned = (A2, B2), (AT, BT)
    G1, V1, W1 = (AT.at[pl.ds(p * L1.rows, L1.rows), :] for p in range(3))

    def chunk_of(c):
        return c * cx + (NC - 1 - c) * (1 - cx)

    def block(i, shift=0, count=W):
        if isinstance(shift, int) and shift % S == 0:
            return pl.ds(pl.multiple_of(i * PR + S + shift, S), count)
        return pl.ds(i * PR + S + shift, count)

    def load(which, k):
        planes = pl.ds(k * CP, CP)
        src, dst = ((u_hbm, A.at[pl.ds(k * CP + 1, CP), pl.ds(S, W), :]), (f_hbm, F.at[planes]))[which]
        return pltpu.make_async_copy(src.at[planes], dst, ld.at[which, k])
    for which in range(2):
        for c in range(NC):
            load(which, chunk_of(c)).start()

    barrier = pltpu.get_barrier_semaphore()
    for p in (px, py, pz):
        pl.semaphore_signal(barrier, inc=1, device_id=p, device_id_type=MESH)
    pl.semaphore_wait(barrier, 3)

    zero = jnp.zeros((S, W), F32)

    def zero_rows(ref2, count):
        @pl.loop(0, count // 64)
        def _(t):
            ref2[pl.ds(pl.multiple_of(t * 64, 64), 64), :] = jnp.zeros((64, W), F32)
        if count % 64:
            ref2[pl.ds(count // 64 * 64, count % 64), :] = jnp.zeros((count % 64, W), F32)
    for ref in (G2, V2, W2, G3, V3, W3):
        zero_rows(ref, ref.shape[0])

    for buf in flats:
        buf[block(129 * cx, -S, PR), :] = jnp.zeros((PR, W), F32)
        for side in (-1, W):
            buf[pl.ds(PR + S + side, N, stride=PR), :] = jnp.zeros((N, W), F32)

    def zero_turned(buf, sides):
        for side in sides:
            buf[pl.ds(S + side, N, stride=PR), :] = jnp.zeros((N, W), F32)
    zero_turned(AT, (-1, W))
    zero_turned(BT, (-1, W))

    @pl.loop(0, XR // S)
    def _(t):
        X[W, eight(pl.multiple_of(t * S, S)), :] = zero
    for q in range(5):
        TS[q, eight(0), :] = zero

    def x_copy(par):
        return pltpu.make_async_remote_copy(
            src_ref=flats[par].at[block(W - LAST * cx), :], dst_ref=flats[par].at[block(129 * cx), :],
            send_sem=xs.at[par], recv_sem=xr.at[par], device_id=px, device_id_type=MESH)

    def side_copy(par, k, src, dst, ssem, rsem, to):
        planes = pl.ds(pl.multiple_of(k * CP, S), CP)
        return pltpu.make_async_remote_copy(
            src_ref=src.at[par, planes, :], dst_ref=dst.at[par, planes, :],
            send_sem=ssem.at[par, k], recv_sem=rsem.at[par, k], device_id=to, device_id_type=MESH)

    def side_copies(par, k):
        return side_copy(par, k, PY, RY, ys, yr, py), side_copy(par, k, PZ, RZ, zs, zr, pz)

    def send(par, k):
        planes = pl.ds(k * CP, CP)
        PY[par, planes, :] = flats[par][pl.ds((k * CP + 1) * PR + S + LAST * (1 - cy), CP, stride=PR), :]
        PZ[par, planes, :] = turned[par][pl.ds(k * CP * PR + S + LAST * (1 - cz), CP, stride=PR), :]
        for cp in side_copies(par, k):
            cp.start()

    def receive(par, k):
        for cp in side_copies(par, k):
            cp.wait()
        planes = pl.ds(k * CP, CP)
        flats[par][pl.ds((k * CP + 1) * PR + S + W - (W + 1) * cy, CP, stride=PR), :] = RY[par, planes, :]
        turned[par][pl.ds(k * CP * PR + S + W - (W + 1) * cz, CP, stride=PR), :] = RZ[par, planes, :]

    def place(g):
        return chunk_of(g // GC) * CP + g % GC * GP

    def turn(par, i0, count):
        for q in range(count):
            turned[par][block(i0 + q), :] = jnp.transpose(flats[par][block(i0 + q + 1), :])

    def side_sums(par, i0):
        for q in range(GP):
            KS[pl.ds(q * W, W), :] = jnp.transpose(turned[par][block(i0 + q, -1), :] + turned[par][block(i0 + q, 1), :])

    def after_chunk(g, done):
        @pl.when((g % GC == 0) & (g > 0))
        def _():
            done(g // GC - 1)

    def first_chunk(par, c):
        @pl.when(c == 0)
        def _():
            x_copy(par).start()

    def stencil_pass(par, visit, dst, done):
        src = flats[par]
        x_copy(par).wait()
        receive(par, chunk_of(0))
        side_sums(par, place(0))

        @pl.loop(0, NG)
        def _(g):
            @pl.when((g % GC == GC - 1) & (g < NG - 1))
            def _():
                receive(par, chunk_of(g // GC + 1))
            i0 = place(g)
            if dst is not None:
                turn(dst, place((g + NG - 1) % NG), GP)
            for t in range(W // RB):
                r = t * RB
                um, uc = src[block(i0, r, RB), :], src[block(i0 + 1, r, RB), :]
                for q in range(GP):
                    un = src[block(i0 + q + 2, r, RB), :]
                    total = (um + un) + (src[block(i0 + q + 1, r - 1, RB), :] + src[block(i0 + q + 1, r + 1, RB), :]) + KS[
                        pl.ds(q * W + r, RB), :]
                    visit(i0 + q, r, uc, total)
                    um, uc = uc, un
            side_sums(par, place((g + 1) % NG))
            if done is not None:
                after_chunk(g, done)
        if dst is not None:
            turn(dst, place(NG - 1), GP)
        if done is not None:
            done(NC - 1)

    def sweep_pass(par, first, last):
        if first:
            for k in range(NC):
                load(1, k).wait()

        def visit(i, r, centre, total):
            fs = F[i, pl.ds(r, RB), :]
            if first:
                fs = fs * F32(h2)
                F[i, pl.ds(r, RB), :] = fs
            flats[1 - par][block(i + 1, r, RB), :] = (3.0 * centre + (total + fs)) * ninth

        def done(c):
            k = chunk_of(c)
            if last:
                store(k).start()
            else:
                first_chunk(1 - par, c)
                send(1 - par, k)
        stencil_pass(par, visit, None if last else 1 - par, done)

    def store(k):
        return pltpu.make_async_copy(B.at[pl.ds(k * CP + 1, CP), pl.ds(S, W), :], out_hbm.at[pl.ds(k * CP, CP)], st.at[k])

    def start_level0():
        @pl.loop(0, NC)
        def _(c):
            k = chunk_of(c)
            load(0, k).wait()

            @pl.loop(0, CP // S)
            def _(t):
                turn(0, k * CP + t * S, S)
            first_chunk(0, c)
            send(0, k)

    def residual_pass():
        def visit(i, r, centre, total):
            BT[block(i, r, RB), :] = F[i, pl.ds(r, RB), :] - 6.0 * centre + total
        stencil_pass(0, visit, None, None)
        zero_turned(BT, (-1,))

    def restrict_planes(i, weights, dst, dst_plane):
        acc = None
        for di, w in weights:
            lo, mid, hi = (BT[pl.ds((i + di) * PR + S + d, 64, stride=2), :] for d in (-1, 0, 1))
            tail = BT[pl.ds((i + di) * PR + S + LAST, 1), :]
            pair = (lo + hi) + 2.0 * mid, tail
            pair = tuple(x if w == 1 else x * w for x in pair)
            acc = pair if acc is None else tuple(x + y for x, y in zip(acc, pair))
        dst[pl.ds(pl.multiple_of(dst_plane * XR, S), 64), :] = acc[0]
        dst[pl.ds(dst_plane * XR + 64, 1), :] = acc[1]

    def restrict_rows():
        restrict_planes(0, ((0, 2.0), (1, 1)), X2, 64 * cx)

        @pl.loop(1, 64)
        def _(i):
            restrict_planes(2 * i, ((-1, 1), (0, 2.0), (1, 1)), X2, i + 64 * cx)
        restrict_planes(LAST, ((0, 1),), XP, 0)

    def gather_chip():
        own = pl.ds(64 * cx, 64)
        cpx = [pltpu.make_async_remote_copy(src_ref=X.at[own], dst_ref=X.at[own], send_sem=cs.at[0], recv_sem=cr.at[0],
                                            device_id=px, device_id_type=MESH),
               pltpu.make_async_remote_copy(src_ref=XP, dst_ref=RXP, send_sem=cs.at[1], recv_sem=cr.at[1],
                                            device_id=px, device_id_type=MESH)]
        for cp in cpx:
            cp.start()
        zero_rows(AT, 3 * L1.rows)
        for cp in cpx:
            cp.wait()
        for t in range(9):
            r = eight(t * S)
            X2[eight(64 * XR + t * S), :] += jnp.where(cx == 0, XP[r, :], RXP[r, :])

    def to_level1():
        @pl.loop(0, 13)
        def _(jo):
          for q in range(5):
            jc = jo * 5 + q
            TS[q, pl.ds(S, W), :] = jnp.transpose(X2[pl.ds(jc, W, stride=XR), :])
            base = (jc + L1.pj) * L1.nk + L1.kp
            lo, mid, hi = (TS[q, pl.ds(S + d, 64, stride=2), :] for d in (-1, 0, 1))
            G1[pl.ds(pl.multiple_of(base, S), 64), :] = ((lo + hi) + 2.0 * mid) * F32(1 / 16)
            G1[pl.ds(base + 64, 1), :] = TS[q, pl.ds(135, 1), :] * F32(1 / 16)

    def wide_exchange(L, G, RYl, SZl, RZl, s):
        cnt = L.h + 1
        js = (L.n - L.h) * (1 - cy)
        cp = pltpu.make_async_remote_copy(
            src_ref=G.at[pl.ds(pl.multiple_of((js + L.pj) * L.nk, S), cnt * L.nk), :], dst_ref=RYl,
            send_sem=cs.at[s], recv_sem=cr.at[s], device_id=py, device_id_type=MESH)
        cp.start()
        cp.wait()
        jd = (L.n * (1 - cy) - L.h * cy + L.pj) * L.nk

        @pl.loop(0, cnt)
        def _(p):
            r = pl.multiple_of(p * L.nk, S)
            G[pl.ds(pl.multiple_of(jd + r, S), L.nk), :] += RYl[pl.ds(r, L.nk), :]
        ks = (L.n - L.h) * (1 - cz) + L.kp
        kd = L.n * (1 - cz) - L.h * cz + L.kp
        jl = L.pj - L.h * cy

        @pl.loop(0, L.n + L.h)
        def _(p):
            SZl[pl.ds(p * cnt, cnt), :] = G[pl.ds((jl + p) * L.nk + ks, cnt), :]
        cp = pltpu.make_async_remote_copy(src_ref=SZl, dst_ref=RZl, send_sem=cs.at[s + 1], recv_sem=cr.at[s + 1],
                                          device_id=pz, device_id_type=MESH)
        cp.start()
        cp.wait()

        @pl.loop(0, L.n + L.h)
        def _(p):
            G[pl.ds((jl + p) * L.nk + kd, cnt), :] += RZl[pl.ds(p * cnt, cnt), :]
            G[pl.ds((jl + p) * L.nk + L.kp - 1 + (L.n + 1) * cz, 1), :] = zero[:1]
        G[pl.ds(pl.multiple_of((L.pj - 1 + (L.n + 1) * cy) * L.nk, S), L.nk), :] = jnp.zeros((L.nk, W), F32)

    def coarse_sum(L, src, r, count):
        lanes = lax.broadcasted_iota(jnp.int32, (count, W), 1)
        c = src[pl.ds(r, count), :]
        left = jnp.where(lanes == 0, 0.0, pltpu.roll(c, 1, 1))
        right = jnp.where(lanes == L.ni - 1, 0.0, pltpu.roll(c, LAST, 1))
        total = (src[pl.ds(r - L.nk, count), :] + src[pl.ds(r + L.nk, count), :]) + (
            src[pl.ds(r - 1, count), :] + src[pl.ds(r + 1, count), :]) + (left + right)
        return c, total

    def coarse_pass(L, src, visit):
        j0 = L.pj - (L.region - L.n) * cy
        k0 = L.kp - L.hb * cz
        count = L.n + L.hb

        @pl.loop(0, L.region // L.unroll)
        def _(po):
            for p in range(L.unroll):
                r = pl.multiple_of((j0 + po * L.unroll + p) * L.nk + k0, S)
                visit(pl.ds(r, count), *coarse_sum(L, src, r, count))

    def first_two(L, G, V):
        def visit(rows, c, total):
            V[rows, :] = (12.0 * c + total) * F32(1 / 81)
        coarse_pass(L, G, visit)

    def smooth(L, G, V, W_):
        def visit(rows, c, total):
            W_[rows, :] = (3.0 * c + (total + G[rows, :])) * ninth
        coarse_pass(L, V, visit)

    def weights(ni, up):
        a = lax.broadcasted_iota(jnp.int32, (W, W), 0)
        b = lax.broadcasted_iota(jnp.int32, (W, W), 1)
        if up:
            fine, coarse = b, a
            w = jnp.where(fine == 2 * coarse, 1.0, 0.0) + jnp.where(
                (fine == 2 * coarse + 1) | (fine == 2 * coarse - 1), 0.5, 0.0)
        else:
            fine, coarse = a, b
            w = jnp.where(fine == 2 * coarse, 2.0, 0.0) + jnp.where(
                (fine == 2 * coarse + 1) | (fine == 2 * coarse - 1), 1.0, 0.0)
        return jnp.where((coarse < ni) & (fine < 2 * ni), w, 0.0).astype(F32)

    def restrict_coarse(L, M, G, V, W_, Gc):
        @pl.loop(0, L.n // 4)
        def _(po):
            for p in range(4):
                r = pl.multiple_of((L.pj + po * 4 + p) * L.nk + L.kp, S)
                c, total = coarse_sum(L, V, r, L.n)
                W_[pl.ds(r, L.n), :] = G[pl.ds(r, L.n), :] - 6.0 * c + total
        for side in (L.pj - 1, L.pj + L.n, L.pj + L.n + 1):
            W_[pl.ds(side * L.nk, L.nk), :] = jnp.zeros((L.nk, W), F32)

        @pl.loop(0, L.n)
        def _(p):
            base = (L.pj + p) * L.nk + L.kp
            W_[eight(pl.multiple_of(base - S, S)), :] = zero
            W_[eight(pl.multiple_of(base + L.n, S)), :] = zero
        w = weights(M.ni, False)

        @pl.loop(0, M.n + 1)
        def _(p):
            base = (L.pj + 2 * p) * L.nk + L.kp
            rows = M.n + 4
            sums = []
            for dj in (-1, 0, 1):
                lo, mid, hi = (W_[pl.ds(base + dj * L.nk + d, rows, stride=2), :] for d in (-1, 0, 1))
                sums.append((lo + hi) + 2.0 * mid)
            T2[pl.ds(p * (M.n + S), rows), :] = (sums[0] + sums[2]) + 2.0 * sums[1]
        hr = M.n + S
        group = (M.n + 1) // (1 + 2 * (M.n // 32))

        @pl.loop(0, (M.n + 1) // group)
        def _(g):
            t0 = pl.multiple_of(g * group * hr, S)
            res = jnp.dot(T2[pl.ds(t0, group * hr), :], w, precision=HI, preferred_element_type=F32) * F32(1 / 16)
            for p in range(group):
                rb = (M.pj + g * group + p) * M.nk + M.kp
                Gc[pl.ds(pl.multiple_of(rb, S), M.n), :] = res[p * hr:p * hr + M.n]
                Gc[pl.ds(rb + M.n, 1), :] = res[p * hr + M.n:p * hr + M.n + 1]

    def prolong_coarse(L, M, V, e):
        w = weights(M.ni, True)
        extra = 3
        j0 = M.pj - extra * cy

        @pl.loop(0, (M.n + extra + 1) // M.group)
        def _(g):
            rows = pl.ds(pl.multiple_of((j0 + g * M.group) * M.nk, S), M.group * M.nk)
            E[rows, :] = jnp.dot(e[rows, :], w, precision=HI, preferred_element_type=F32)

        @pl.loop(0, M.n + extra)
        def _(p):
            jc = j0 + p - M.pj
            fb = (L.pj + 2 * jc) * L.nk + L.kp
            eb = (j0 + p) * M.nk + M.kp
            for kc, rows in ((0, M.n), (M.n * (1 - cz) - 4 * cz, 4)):
                a, b = E[pl.ds(eb + kc, rows), :], E[pl.ds(eb + kc + 1, rows), :]
                c, d = E[pl.ds(eb + M.nk + kc, rows), :], E[pl.ds(eb + M.nk + kc + 1, rows), :]
                ab = a + b
                f = fb + 2 * kc
                V[pl.ds(f, rows, stride=2), :] += a
                V[pl.ds(f + 1, rows, stride=2), :] += 0.5 * ab
                V[pl.ds(f + L.nk, rows, stride=2), :] += 0.5 * (a + c)
                V[pl.ds(f + L.nk + 1, rows, stride=2), :] += 0.25 * (ab + (c + d))

    def from_level1():
        @pl.loop(0, 13)
        def _(jo):
          for q in range(5):
            jc = jo * 5 + q
            base = (jc + L1.pj) * L1.nk + L1.kp
            a, b = V1[pl.ds(pl.multiple_of(base, S), 64), :], V1[pl.ds(base + 1, 64), :]
            TS[q, pl.ds(S, 64, stride=2), :] = a
            TS[q, pl.ds(S + 1, 64, stride=2), :] = 0.5 * (a + b)
            X2[pl.ds(jc, W, stride=XR), :] = jnp.transpose(TS[q, pl.ds(S, W), :])

    def prolong_level0():
        zero_turned(AT, (-1, W))

        def done(c):
            first_chunk(1, c)
            send(1, chunk_of(c))

        @pl.loop(0, NG)
        def _(g):
            i0 = place(g)
            turn(1, place((g + NG - 1) % NG), GP)
            for q in range(GP // 2):
                half = W // 2
                xb = (i0 // 2 + q + half * cx) * XR
                a, b = X2[pl.ds(xb, half), :], X2[pl.ds(xb + 1, half), :]
                cc, d = X2[pl.ds(xb + XR, half), :], X2[pl.ds(xb + XR + 1, half), :]
                ab = a + b
                f = (i0 + 2 * q + 1) * PR + S
                for shift, value in ((0, a), (1, 0.5 * ab), (PR, 0.5 * (a + cc)), (PR + 1, 0.25 * (ab + (cc + d)))):
                    rows = pl.ds(f + shift, half, stride=2)
                    B2[rows, :] = A2[rows, :] + value
            after_chunk(g, done)
        turn(1, place(NG - 1), GP)
        done(NC - 1)

    def smooth_coarsest():
        @pl.loop(0, 7)
        def _(s):
            smooth(L3, G3, V3, W3)
            smooth(L3, G3, W3, V3)

    start_level0()
    sweep_pass(0, True, False)
    sweep_pass(1, False, False)
    residual_pass()
    restrict_rows()
    gather_chip()
    to_level1()
    wide_exchange(L1, G1, RY1, SZ1, RZ1, 2)
    first_two(L1, G1, V1)
    restrict_coarse(L1, L2, G1, V1, W1, G2)
    wide_exchange(L2, G2, RY2, SZ2, RZ2, 4)
    first_two(L2, G2, V2)
    restrict_coarse(L2, L3, G2, V2, W2, G3)
    wide_exchange(L3, G3, RY3, SZ3, RZ3, 6)
    first_two(L3, G3, V3)
    smooth_coarsest()
    prolong_coarse(L2, L3, V2, V3)
    smooth(L2, G2, V2, W2)
    smooth(L2, G2, W2, V2)
    prolong_coarse(L1, L2, V1, V2)
    smooth(L1, G1, V1, W1)
    smooth(L1, G1, W1, V1)
    from_level1()
    prolong_level0()
    sweep_pass(1, False, False)
    sweep_pass(0, False, True)
    for k in range(NC):
        store(k).wait()


def solution(mesh):
    spec = P(('dp', 'sx'), 'sy', 'sz')

    def local(f, u):
        size = 2 * f.shape[1]
        h2 = 1.0 / float((size + 1) ** 2)
        vm = lambda *s: pltpu.VMEM(s, F32)
        scratch = [vm(130, PR, W), vm(130, PR, W), vm(N * PR, W), vm(N * PR, W), vm(N, N, W), vm(129, XR, W),
                   vm(XR, W), vm(XR, W), vm(5, 136, W), vm(GP * W, W), vm(2, N, W), vm(2, N, W), vm(2, N, W), vm(2, N, W)]
        for L in LEVS[1:]:
            scratch += [vm(L.rows, W)] * 3
        scratch += [vm(max(L2.rows, L3.rows), W), vm(33 * 40, W)]
        for L in LEVS:
            z = up8((L.n + L.h) * (L.h + 1))
            scratch += [vm((L.h + 1) * L.nk, W), vm(z, W), vm(z, W)]
        dma = pltpu.SemaphoreType.DMA
        scratch += [dma((2, NC)), dma((NC,)), dma((2,)), dma((2,)), dma((2, NC)), dma((2, NC)), dma((2, NC)), dma((2, NC)),
                    dma((S,)), dma((S,))]
        return pl.pallas_call(
            functools.partial(body, h2),
            out_shape=jax.ShapeDtypeStruct(f.shape, F32),
            in_specs=[pl.BlockSpec(memory_space=pl.ANY)] * 2,
            out_specs=pl.BlockSpec(memory_space=pl.ANY),
            scratch_shapes=scratch,
            compiler_params=pltpu.CompilerParams(collective_id=0, has_side_effects=True, vmem_limit_bytes=67043328),
        )(f, u)

    def run(rhs_grid, u_start):
        return jax.shard_map(local, mesh=mesh, in_specs=(spec, spec), out_specs=spec, check_vma=False)(rhs_grid, u_start)
    return run
```

time: 163 us -> 135 us (0.83)
  Pallas kernels: 155 us -> 127 us
    pallas_call x1, Pallas kernels: 155 us -> 127 us  [local(): pl.pallas_call(functools.partial(body, h2), out_shape=jax.ShapeDtypeStruc...]
where the time goes in v2:
time: 135 us
  Pallas kernels  127 us (94%)
  local copies, waits for them, and re-layouts  7.89 us (6%)
    pallas_call x1, Pallas kernels, local(): pl.pallas_call(functools.partial(body, h2), out_shape=jax.ShapeDtypeStruc...  127 us
    unnamed x1, local copies, waits for them, and re-layouts  7.89 us

profile of v2, /device:TPU:0, one launch (start us, length us, event | category | flops | bytes accessed | tf_op | source)
XLA Modules:
  0.0 134.8 jit_solution(5948347910726806794)
XLA Ops:
  0.0 126.9 %shard_map.28 = f32[128,128,128]{2,1,0:T(8,128)} custom-call(f32[128,128,128]{2,1,0:T(8,128)} %f_hbm.1, f32[128,128,128]{2,1,0:T(8,128)} %u_hbm.1), custom_call_target="tpu_custom_call" | custom-call | tf_op jit(solution)/shard_map/pallas_call | solution.py:508
  126.9 7.9 %copy.4 = f32[128,128,128]{2,1,0:T(8,128)} copy(f32[128,128,128]{2,1,0:T(8,128)} %shard_map.28) | data formatting | bytes 16777216

commit v3 on v2

--- a/solution.py
+++ b/solution.py
@@ -34,7 +34,7 @@
 L1 = Lev(64, 4, 6, 8, 8, 128, 68, 4, 1)
 L2 = Lev(32, 5, 10, 8, 8, 64, 40, 8, 12)
 L3 = Lev(16, 16, 18, 16, 16, 32, 32, 8, 10)
-LEVS = (L1, L2, L3)
+EXTRA = 3
 
 
 def up8(x):
@@ -47,12 +47,12 @@
 
 def body(h2, f_hbm, u_hbm, out_hbm, A, B, AT, BT, F, X, XP, RXP, TS, KS, PZ, RZ, PY, RY,
          G2, V2, W2, G3, V3, W3, E, T2,
-         RY1, SZ1, RZ1, RY2, SZ2, RZ2, RY3, SZ3, RZ3,
+         RY1, SZ1, RZ1, RY2, SZ2, RZ2, S3, R3,
          ld, st, xs, xr, zs, zr, ys, yr, cs, cr):
     cx, cy, cz = lax.axis_index('sx'), lax.axis_index('sy'), lax.axis_index('sz')
     ninth = F32(1.0 / 9.0)
     px, py, pz = {'sx': 1 - cx}, {'sy': 1 - cy}, {'sz': 1 - cz}
-    bufs = (A, B)
+    pyz = {**py, **pz}
 
     def flat(ref):
         return ref.reshape(ref.shape[0] * ref.shape[1], ref.shape[2])
@@ -78,9 +78,9 @@
             load(which, chunk_of(c)).start()
 
     barrier = pltpu.get_barrier_semaphore()
-    for p in (px, py, pz):
+    for p in (px, py, pz, pyz):
         pl.semaphore_signal(barrier, inc=1, device_id=p, device_id_type=MESH)
-    pl.semaphore_wait(barrier, 3)
+    pl.semaphore_wait(barrier, 4)
 
     zero = jnp.zeros((S, W), F32)
 
@@ -339,20 +339,18 @@
             W_[rows, :] = (3.0 * c + (total + G[rows, :])) * ninth
         coarse_pass(L, V, visit)
 
-    def weights(ni, up):
+    def weights(ni, up, offset=0):
         a = lax.broadcasted_iota(jnp.int32, (W, W), 0)
         b = lax.broadcasted_iota(jnp.int32, (W, W), 1)
-        if up:
-            fine, coarse = b, a
-            w = jnp.where(fine == 2 * coarse, 1.0, 0.0) + jnp.where(
-                (fine == 2 * coarse + 1) | (fine == 2 * coarse - 1), 0.5, 0.0)
-        else:
-            fine, coarse = a, b
-            w = jnp.where(fine == 2 * coarse, 2.0, 0.0) + jnp.where(
-                (fine == 2 * coarse + 1) | (fine == 2 * coarse - 1), 1.0, 0.0)
-        return jnp.where((coarse < ni) & (fine < 2 * ni), w, 0.0).astype(F32)
-
-    def restrict_coarse(L, M, G, V, W_, Gc):
+        fine, coarse = (b, a - offset) if up else (a, b - offset)
+        near = (fine == 2 * coarse + 1) | (fine == 2 * coarse - 1)
+        w = jnp.where(fine == 2 * coarse, 1.0, 0.0) + jnp.where(near, 0.5, 0.0)
+        return jnp.where((coarse >= 0) & (coarse < ni) & (fine < 2 * ni), w if up else 2.0 * w, 0.0).astype(F32)
+
+    def lane_dot(x, w):
+        return jnp.dot(x, w, precision=HI, preferred_element_type=F32)
+
+    def restrict_coarse(L, M, G, V, W_):
         @pl.loop(0, L.n // 4)
         def _(po):
             for p in range(4):
@@ -367,7 +365,6 @@
             base = (L.pj + p) * L.nk + L.kp
             W_[eight(pl.multiple_of(base - S, S)), :] = zero
             W_[eight(pl.multiple_of(base + L.n, S)), :] = zero
-        w = weights(M.ni, False)
 
         @pl.loop(0, M.n + 1)
         def _(p):
@@ -378,29 +375,93 @@
                 lo, mid, hi = (W_[pl.ds(base + dj * L.nk + d, rows, stride=2), :] for d in (-1, 0, 1))
                 sums.append((lo + hi) + 2.0 * mid)
             T2[pl.ds(p * (M.n + S), rows), :] = (sums[0] + sums[2]) + 2.0 * sums[1]
+
+    def restrict_lanes(M, Gc):
         hr = M.n + S
-        group = (M.n + 1) // (1 + 2 * (M.n // 32))
+        group = 11
+        w = weights(M.ni, False)
 
         @pl.loop(0, (M.n + 1) // group)
         def _(g):
             t0 = pl.multiple_of(g * group * hr, S)
-            res = jnp.dot(T2[pl.ds(t0, group * hr), :], w, precision=HI, preferred_element_type=F32) * F32(1 / 16)
+            res = lane_dot(T2[pl.ds(t0, group * hr), :], w) * F32(1 / 16)
             for p in range(group):
                 rb = (M.pj + g * group + p) * M.nk + M.kp
                 Gc[pl.ds(pl.multiple_of(rb, S), M.n), :] = res[p * hr:p * hr + M.n]
                 Gc[pl.ds(rb + M.n, 1), :] = res[p * hr + M.n:p * hr + M.n + 1]
 
-    def prolong_coarse(L, M, V, e):
+    KR, KA = 48, 32
+
+    def gather_coarsest():
+        hr, cells = L3.n + S, L3.n + 1
+        parts = [lane_dot(T2[pl.ds(p * S * hr, n * hr), :], weights(L3.ni, False, L3.ni * (2 * cy + p)))
+                 for p, n in ((0, S), (1, S), (2, 1))]
+        for p in range(S):
+            x = parts[0][p * hr:p * hr + cells] + parts[1][p * hr:p * hr + cells]
+            x = x + parts[2][:cells] if p == 0 else x
+            S3[pl.ds(p * cells, cells), :] = x * F32(1 / 16)
+        cps = [pltpu.make_async_remote_copy(src_ref=S3, dst_ref=R3.at[n], send_sem=cs.at[6 + n],
+                                            recv_sem=cr.at[6 + n], device_id=to, device_id_type=MESH)
+               for n, to in enumerate((py, pz, pyz))]
+        for cp in cps:
+            cp.start()
+        for cp in cps:
+            cp.wait()
+        low, high = S + L3.n * cz, S + L3.n * (1 - cz)
+        for p in range(S):
+            rows = pl.ds(p * cells, cells)
+            G3[pl.ds(p * KR + low, cells), :] += S3[rows, :] + R3[0, rows, :]
+            G3[pl.ds(p * KR + high, cells), :] += R3[1, rows, :] + R3[2, rows, :]
+            G3[pl.ds(p * KR + S + KA, 1), :] = zero[:1]
+
+    def coarsest_pass(src, visit):
+        lanes = lax.broadcasted_iota(jnp.int32, (KA, W), 1)
+        cell = lanes % KA
+        at = lambda p: pl.ds(p * KR + S, KA)
+        for p in range(S):
+            c = src[at(p), :]
+            left = jnp.where(cell == 0, 0.0, pltpu.roll(c, 1, 1))
+            right = jnp.where(cell == KA - 1, 0.0, pltpu.roll(c, LAST, 1))
+            lo = src[at(p - 1), :] if p else jnp.where(lanes < KA, 0.0, pltpu.roll(src[at(S - 1), :], KA, 1))
+            hi = src[at(p + 1), :] if p < S - 1 else jnp.where(lanes < W - KA, pltpu.roll(src[at(0), :], W - KA, 1), 0.0)
+            total = (lo + hi) + (src[pl.ds(p * KR + S - 1, KA), :] + src[pl.ds(p * KR + S + 1, KA), :]) + (left + right)
+            visit(at(p), c, total)
+
+    def solve_coarsest():
+        def first(rows, c, total):
+            V3[rows, :] = (12.0 * c + total) * F32(1 / 81)
+        coarsest_pass(G3, first)
+
+        @pl.loop(0, 7)
+        def _(s):
+            for V, W_ in ((V3, W3), (W3, V3)):
+                def visit(rows, c, total):
+                    W_[rows, :] = (3.0 * c + (total + G3[rows, :])) * ninth
+                coarsest_pass(V, visit)
+
+    def spread_coarsest():
+        def plane(j):
+            return pl.ds(pl.multiple_of((L3.pj + j) * L3.nk + L3.kp - S, S), KA)
+        E[plane(L3.n), :] = jnp.zeros((KA, W), F32)
+        x = jnp.concatenate([V3[pl.ds(pl.multiple_of(p * KR + L3.n * cz, S), KA), :] for p in range(S)], axis=0)
+        for q in (0, 1, 2 - 3 * cy):
+            y = lane_dot(x, weights(L3.ni, True, L3.ni * (2 * cy + q)))
+            for p in range(S):
+                E[plane(q * S + p), :] = y[p * KA:p * KA + KA]
+
+    def spread_lanes(M, e):
         w = weights(M.ni, True)
-        extra = 3
-        j0 = M.pj - extra * cy
-
-        @pl.loop(0, (M.n + extra + 1) // M.group)
+        j0 = M.pj - EXTRA * cy
+
+        @pl.loop(0, (M.n + EXTRA + 1) // M.group)
         def _(g):
             rows = pl.ds(pl.multiple_of((j0 + g * M.group) * M.nk, S), M.group * M.nk)
-            E[rows, :] = jnp.dot(e[rows, :], w, precision=HI, preferred_element_type=F32)
-
-        @pl.loop(0, M.n + extra)
+            E[rows, :] = lane_dot(e[rows, :], w)
+
+    def prolong_coarse(L, M, V):
+        j0 = M.pj - EXTRA * cy
+
+        @pl.loop(0, M.n + EXTRA)
         def _(p):
             jc = j0 + p - M.pj
             fb = (L.pj + 2 * jc) * L.nk + L.kp
@@ -451,12 +512,6 @@
         turn(1, place(NG - 1), GP)
         done(NC - 1)
 
-    def smooth_coarsest():
-        @pl.loop(0, 7)
-        def _(s):
-            smooth(L3, G3, V3, W3)
-            smooth(L3, G3, W3, V3)
-
     start_level0()
     sweep_pass(0, True, False)
     sweep_pass(1, False, False)
@@ -466,17 +521,19 @@
     to_level1()
     wide_exchange(L1, G1, RY1, SZ1, RZ1, 2)
     first_two(L1, G1, V1)
-    restrict_coarse(L1, L2, G1, V1, W1, G2)
+    restrict_coarse(L1, L2, G1, V1, W1)
+    restrict_lanes(L2, G2)
     wide_exchange(L2, G2, RY2, SZ2, RZ2, 4)
     first_two(L2, G2, V2)
-    restrict_coarse(L2, L3, G2, V2, W2, G3)
-    wide_exchange(L3, G3, RY3, SZ3, RZ3, 6)
-    first_two(L3, G3, V3)
-    smooth_coarsest()
-    prolong_coarse(L2, L3, V2, V3)
+    restrict_coarse(L2, L3, G2, V2, W2)
+    gather_coarsest()
+    solve_coarsest()
+    spread_coarsest()
+    prolong_coarse(L2, L3, V2)
     smooth(L2, G2, V2, W2)
     smooth(L2, G2, W2, V2)
-    prolong_coarse(L1, L2, V1, V2)
+    spread_lanes(L2, V2)
+    prolong_coarse(L1, L2, V1)
     smooth(L1, G1, V1, W1)
     smooth(L1, G1, W1, V1)
     from_level1()
@@ -496,15 +553,15 @@
         vm = lambda *s: pltpu.VMEM(s, F32)
         scratch = [vm(130, PR, W), vm(130, PR, W), vm(N * PR, W), vm(N * PR, W), vm(N, N, W), vm(129, XR, W),
                    vm(XR, W), vm(XR, W), vm(5, 136, W), vm(GP * W, W), vm(2, N, W), vm(2, N, W), vm(2, N, W), vm(2, N, W)]
-        for L in LEVS[1:]:
-            scratch += [vm(L.rows, W)] * 3
+        scratch += [vm(L2.rows, W)] * 3 + [vm(S * 48, W)] * 3
         scratch += [vm(max(L2.rows, L3.rows), W), vm(33 * 40, W)]
-        for L in LEVS:
+        for L in (L1, L2):
             z = up8((L.n + L.h) * (L.h + 1))
             scratch += [vm((L.h + 1) * L.nk, W), vm(z, W), vm(z, W)]
+        scratch += [vm(S * (L3.n + 1), W), vm(3, S * (L3.n + 1), W)]
         dma = pltpu.SemaphoreType.DMA
         scratch += [dma((2, NC)), dma((NC,)), dma((2,)), dma((2,)), dma((2, NC)), dma((2, NC)), dma((2, NC)), dma((2, NC)),
-                    dma((S,)), dma((S,))]
+                    dma((S + 1,)), dma((S + 1,))]
         return pl.pallas_call(
             functools.partial(body, h2),
             out_shape=jax.ShapeDtypeStruct(f.shape, F32),

time: 135 us -> 118 us (0.87)
  Pallas kernels: 127 us -> 110 us
    pallas_call x1, Pallas kernels: 127 us -> 110 us  [local(): pl.pallas_call(functools.partial(body, h2), out_shape=jax.ShapeDtypeStruc...]
where the time goes in v3:
time: 118 us
  Pallas kernels  110 us (93%)
  local copies, waits for them, and re-layouts  7.89 us (7%)
    pallas_call x1, Pallas kernels, local(): pl.pallas_call(functools.partial(body, h2), out_shape=jax.ShapeDtypeStruc...  110 us
    unnamed x1, local copies, waits for them, and re-layouts  7.89 us

profile of v3, /device:TPU:0, one launch (start us, length us, event | category | flops | bytes accessed | tf_op | source)
XLA Modules:
  0.0 117.5 jit_solution(10259611416612823944)
XLA Ops:
  0.0 109.6 %shard_map.28 = f32[128,128,128]{2,1,0:T(8,128)} custom-call(f32[128,128,128]{2,1,0:T(8,128)} %f_hbm.1, f32[128,128,128]{2,1,0:T(8,128)} %u_hbm.1), custom_call_target="tpu_custom_call" | custom-call | tf_op jit(solution)/shard_map/pallas_call | solution.py:565
  109.7 7.9 %copy.4 = f32[128,128,128]{2,1,0:T(8,128)} copy(f32[128,128,128]{2,1,0:T(8,128)} %shard_map.28) | data formatting | bytes 16777216

commit v4 on v3

--- a/solution.py
+++ b/solution.py
@@ -11,7 +11,7 @@
 NC = 4
 XR = 72
 CP = N // NC
-GP = 4
+GP = 8
 GC = CP // GP
 NG = N // GP
 RB = 32
@@ -46,8 +46,8 @@
 
 
 def body(h2, f_hbm, u_hbm, out_hbm, A, B, AT, BT, F, X, XP, RXP, TS, KS, PZ, RZ, PY, RY,
-         G2, V2, W2, G3, V3, W3, E, T2,
-         RY1, SZ1, RZ1, RY2, SZ2, RZ2, S3, R3,
+         V1, W1, G2, V2, W2, G3, V3, W3,
+         SY1, RY1, SZ1, RZ1, SD1, RD1, SY2, RY2, SZ2, RZ2, SD2, RD2, S3, R3,
          ld, st, xs, xr, zs, zr, ys, yr, cs, cr):
     cx, cy, cz = lax.axis_index('sx'), lax.axis_index('sy'), lax.axis_index('sz')
     ninth = F32(1.0 / 9.0)
@@ -59,7 +59,8 @@
 
     A2, B2, X2 = flat(A), flat(B), flat(X)
     flats, turned = (A2, B2), (AT, BT)
-    G1, V1, W1 = (AT.at[pl.ds(p * L1.rows, L1.rows), :] for p in range(3))
+    G1, T2 = AT.at[pl.ds(0, L1.rows), :], AT.at[pl.ds(L1.rows, 33 * 40), :]
+    E = AT.at[pl.ds(L1.rows + 33 * 40, max(L2.rows, L3.rows)), :]
 
     def chunk_of(c):
         return c * cx + (NC - 1 - c) * (1 - cx)
@@ -90,7 +91,7 @@
             ref2[pl.ds(pl.multiple_of(t * 64, 64), 64), :] = jnp.zeros((64, W), F32)
         if count % 64:
             ref2[pl.ds(count // 64 * 64, count % 64), :] = jnp.zeros((count % 64, W), F32)
-    for ref in (G2, V2, W2, G3, V3, W3):
+    for ref in (V1, W1, G2, V2, W2, G3, V3, W3):
         zero_rows(ref, ref.shape[0])
 
     for buf in flats:
@@ -232,102 +233,132 @@
         stencil_pass(0, visit, None, None)
         zero_turned(BT, (-1,))
 
-    def restrict_planes(i, weights, dst, dst_plane):
+    def restrict_planes(i, weights, dst, dst_plane, jc, count):
         acc = None
         for di, w in weights:
-            lo, mid, hi = (BT[pl.ds((i + di) * PR + S + d, 64, stride=2), :] for d in (-1, 0, 1))
-            tail = BT[pl.ds((i + di) * PR + S + LAST, 1), :]
-            pair = (lo + hi) + 2.0 * mid, tail
-            pair = tuple(x if w == 1 else x * w for x in pair)
-            acc = pair if acc is None else tuple(x + y for x, y in zip(acc, pair))
-        dst[pl.ds(pl.multiple_of(dst_plane * XR, S), 64), :] = acc[0]
-        dst[pl.ds(dst_plane * XR + 64, 1), :] = acc[1]
-
-    def restrict_rows():
-        restrict_planes(0, ((0, 2.0), (1, 1)), X2, 64 * cx)
+            base = (i + di) * PR + S + 2 * jc
+            lo, mid, hi = (BT[pl.ds(base + d, count, stride=2), :] for d in (-1, 0, 1))
+            tail = BT[pl.ds(base - 1, 1), :]
+            pair = (lo + hi) + 2.0 * mid if count > 1 else tail
+            pair = pair if w == 1 else pair * w
+            acc = pair if acc is None else acc + pair
+        dst[pl.ds(dst_plane * XR + jc, count), :] = acc
+
+    def restrict_rows(jc, count):
+        restrict_planes(0, ((0, 2.0), (1, 1)), X2, 64 * cx, jc, count)
 
         @pl.loop(1, 64)
         def _(i):
-            restrict_planes(2 * i, ((-1, 1), (0, 2.0), (1, 1)), X2, i + 64 * cx)
-        restrict_planes(LAST, ((0, 1),), XP, 0)
-
-    def gather_chip():
+            restrict_planes(2 * i, ((-1, 1), (0, 2.0), (1, 1)), X2, i + 64 * cx, jc, count)
+
+    JP = (24, 24, 16)
+
+    def to_level1():
+        spans = []
+        for m, count in enumerate(JP):
+            jc = sum(JP[:m])
+            pieces = ((jc, count),) if m < 2 else ((jc, count), (jc + count, 1))
+            spans.append((jc, pieces))
+        for jc, pieces in spans:
+            for piece in pieces:
+                restrict_planes(LAST, ((0, 1),), XP, 0, *piece)
         own = pl.ds(64 * cx, 64)
-        cpx = [pltpu.make_async_remote_copy(src_ref=X.at[own], dst_ref=X.at[own], send_sem=cs.at[0], recv_sem=cr.at[0],
-                                            device_id=px, device_id_type=MESH),
-               pltpu.make_async_remote_copy(src_ref=XP, dst_ref=RXP, send_sem=cs.at[1], recv_sem=cr.at[1],
-                                            device_id=px, device_id_type=MESH)]
-        for cp in cpx:
-            cp.start()
-        zero_rows(AT, 3 * L1.rows)
-        for cp in cpx:
-            cp.wait()
-        for t in range(9):
-            r = eight(t * S)
-            X2[eight(64 * XR + t * S), :] += jnp.where(cx == 0, XP[r, :], RXP[r, :])
-
-    def to_level1():
-        @pl.loop(0, 13)
-        def _(jo):
-          for q in range(5):
-            jc = jo * 5 + q
+        whole = [pltpu.make_async_remote_copy(src_ref=XP, dst_ref=RXP, send_sem=cs.at[3], recv_sem=cr.at[3],
+                                              device_id=px, device_id_type=MESH)]
+        whole[0].start()
+        for m, (jc, pieces) in enumerate(spans):
+            for piece in pieces:
+                restrict_rows(*piece)
+            part = X.at[own, pl.ds(jc, JP[0]), :]
+            whole.append(pltpu.make_async_remote_copy(src_ref=part, dst_ref=part, send_sem=cs.at[m], recv_sem=cr.at[m],
+                                                      device_id=px, device_id_type=MESH))
+            whole[-1].start()
+        zero_rows(AT, L1.rows)
+        whole[0].wait()
+
+        def tile(jc, q):
             TS[q, pl.ds(S, W), :] = jnp.transpose(X2[pl.ds(jc, W, stride=XR), :])
             base = (jc + L1.pj) * L1.nk + L1.kp
             lo, mid, hi = (TS[q, pl.ds(S + d, 64, stride=2), :] for d in (-1, 0, 1))
             G1[pl.ds(pl.multiple_of(base, S), 64), :] = ((lo + hi) + 2.0 * mid) * F32(1 / 16)
             G1[pl.ds(base + 64, 1), :] = TS[q, pl.ds(135, 1), :] * F32(1 / 16)
 
-    def wide_exchange(L, G, RYl, SZl, RZl, s):
-        cnt = L.h + 1
-        js = (L.n - L.h) * (1 - cy)
-        cp = pltpu.make_async_remote_copy(
-            src_ref=G.at[pl.ds(pl.multiple_of((js + L.pj) * L.nk, S), cnt * L.nk), :], dst_ref=RYl,
-            send_sem=cs.at[s], recv_sem=cr.at[s], device_id=py, device_id_type=MESH)
-        cp.start()
-        cp.wait()
-        jd = (L.n * (1 - cy) - L.h * cy + L.pj) * L.nk
-
-        @pl.loop(0, cnt)
+        for m, (jc, pieces) in enumerate(spans):
+            whole[m + 1].wait()
+            rows = pl.ds(jc, JP[0])
+            X2[pl.ds(64 * XR + jc, JP[0]), :] += jnp.where(cx == 0, XP[rows, :], RXP[rows, :])
+
+            @pl.loop(0, JP[m] // 4)
+            def _(jo):
+                for q in range(4):
+                    tile(jc + jo * 4 + q, q)
+        tile(64, 4)
+
+    def wide_exchange(L, G, SY, RY_, SZ, RZ_, SD, RD, s):
+        cnt, wide = L.h, L.n + S
+        js, ks = (L.n + 1 - cnt) * (1 - cy) + L.pj, (L.n + 1 - cnt) * (1 - cz) + L.kp
+        jd, kd = L.n * (1 - cy) + (1 - cnt) * cy + L.pj, L.n * (1 - cz) + (1 - cnt) * cz + L.kp
+        for p in range(cnt):
+            SY[pl.ds(p * wide, wide), :] = G[pl.ds(pl.multiple_of((js + p) * L.nk + L.kp, S), wide), :]
+            SD[pl.ds(p * S, cnt), :] = G[pl.ds((js + p) * L.nk + ks, cnt), :]
+        cps = [pltpu.make_async_remote_copy(src_ref=src, dst_ref=dst, send_sem=cs.at[s + n], recv_sem=cr.at[s + n],
+                                            device_id=to, device_id_type=MESH)
+               for n, (src, dst, to) in enumerate(((SY, RY_, py), (SD, RD, pyz), (SZ, RZ_, pz)))]
+        cps[0].start()
+        cps[1].start()
+
+        @pl.loop(0, L.n + 1)
         def _(p):
-            r = pl.multiple_of(p * L.nk, S)
-            G[pl.ds(pl.multiple_of(jd + r, S), L.nk), :] += RYl[pl.ds(r, L.nk), :]
-        ks = (L.n - L.h) * (1 - cz) + L.kp
-        kd = L.n * (1 - cz) - L.h * cz + L.kp
-        jl = L.pj - L.h * cy
-
-        @pl.loop(0, L.n + L.h)
+            SZ[pl.ds(p * cnt, cnt), :] = G[pl.ds((L.pj + p) * L.nk + ks, cnt), :]
+        cps[2].start()
+        for cp in cps:
+            cp.wait()
+        for p in range(cnt):
+            G[pl.ds(pl.multiple_of((jd + p) * L.nk + L.kp, S), wide), :] += RY_[pl.ds(p * wide, wide), :]
+            G[pl.ds((jd + p) * L.nk + kd, cnt), :] += RD[pl.ds(p * S, cnt), :]
+
+        @pl.loop(0, L.n + 1)
         def _(p):
-            SZl[pl.ds(p * cnt, cnt), :] = G[pl.ds((jl + p) * L.nk + ks, cnt), :]
-        cp = pltpu.make_async_remote_copy(src_ref=SZl, dst_ref=RZl, send_sem=cs.at[s + 1], recv_sem=cr.at[s + 1],
-                                          device_id=pz, device_id_type=MESH)
-        cp.start()
-        cp.wait()
-
-        @pl.loop(0, L.n + L.h)
+            G[pl.ds((L.pj + p) * L.nk + kd, cnt), :] += RZ_[pl.ds(p * cnt, cnt), :]
+        last = L.kp - 1 + (L.n + 1) * cz
+
+        @pl.loop(0, L.region)
         def _(p):
-            G[pl.ds((jl + p) * L.nk + kd, cnt), :] += RZl[pl.ds(p * cnt, cnt), :]
-            G[pl.ds((jl + p) * L.nk + L.kp - 1 + (L.n + 1) * cz, 1), :] = zero[:1]
+            G[pl.ds((L.pj - (L.region - L.n) * cy + p) * L.nk + last, 1), :] = zero[:1]
         G[pl.ds(pl.multiple_of((L.pj - 1 + (L.n + 1) * cy) * L.nk, S), L.nk), :] = jnp.zeros((L.nk, W), F32)
 
-    def coarse_sum(L, src, r, count):
+    def coarse_pass(L, src, visit, own=False):
+        j0 = L.pj if own else L.pj - (L.region - L.n) * cy
+        k0 = L.kp if own else L.kp - L.hb * cz
+        count = L.n if own else L.n + L.hb
+        groups = (L.n if own else L.region) // L.unroll
         lanes = lax.broadcasted_iota(jnp.int32, (count, W), 1)
-        c = src[pl.ds(r, count), :]
-        left = jnp.where(lanes == 0, 0.0, pltpu.roll(c, 1, 1))
-        right = jnp.where(lanes == L.ni - 1, 0.0, pltpu.roll(c, LAST, 1))
-        total = (src[pl.ds(r - L.nk, count), :] + src[pl.ds(r + L.nk, count), :]) + (
-            src[pl.ds(r - 1, count), :] + src[pl.ds(r + 1, count), :]) + (left + right)
-        return c, total
-
-    def coarse_pass(L, src, visit):
-        j0 = L.pj - (L.region - L.n) * cy
-        k0 = L.kp - L.hb * cz
-        count = L.n + L.hb
-
-        @pl.loop(0, L.region // L.unroll)
-        def _(po):
+
+        def place(g, p):
+            return pl.multiple_of((j0 + g * L.unroll + p) * L.nk + k0, S)
+
+        def sides(g):
+            out = []
             for p in range(L.unroll):
-                r = pl.multiple_of((j0 + po * L.unroll + p) * L.nk + k0, S)
-                visit(pl.ds(r, count), *coarse_sum(L, src, r, count))
+                c = src[pl.ds(place(g, p), count), :]
+                out.append(jnp.where(lanes == 0, 0.0, pltpu.roll(c, 1, 1)) + jnp.where(
+                    lanes == L.ni - 1, 0.0, pltpu.roll(c, LAST, 1)))
+            return out
+
+        def keep(sums):
+            for p in range(L.unroll):
+                KS[pl.ds(p * count, count), :] = sums[p]
+        keep(sides(0))
+
+        @pl.loop(0, groups)
+        def _(g):
+            later = sides((g + 1) % groups)
+            for p in range(L.unroll):
+                r = place(g, p)
+                total = (src[pl.ds(r - L.nk, count), :] + src[pl.ds(r + L.nk, count), :]) + (
+                    src[pl.ds(r - 1, count), :] + src[pl.ds(r + 1, count), :]) + KS[pl.ds(p * count, count), :]
+                visit(pl.ds(r, count), src[pl.ds(r, count), :], total)
+            keep(later)
 
     def first_two(L, G, V):
         def visit(rows, c, total):
@@ -351,12 +382,9 @@
         return jnp.dot(x, w, precision=HI, preferred_element_type=F32)
 
     def restrict_coarse(L, M, G, V, W_):
-        @pl.loop(0, L.n // 4)
-        def _(po):
-            for p in range(4):
-                r = pl.multiple_of((L.pj + po * 4 + p) * L.nk + L.kp, S)
-                c, total = coarse_sum(L, V, r, L.n)
-                W_[pl.ds(r, L.n), :] = G[pl.ds(r, L.n), :] - 6.0 * c + total
+        def visit(rows, c, total):
+            W_[rows, :] = G[rows, :] - 6.0 * c + total
+        coarse_pass(L, V, visit, True)
         for side in (L.pj - 1, L.pj + L.n, L.pj + L.n + 1):
             W_[pl.ds(side * L.nk, L.nk), :] = jnp.zeros((L.nk, W), F32)
 
@@ -400,8 +428,8 @@
             x = parts[0][p * hr:p * hr + cells] + parts[1][p * hr:p * hr + cells]
             x = x + parts[2][:cells] if p == 0 else x
             S3[pl.ds(p * cells, cells), :] = x * F32(1 / 16)
-        cps = [pltpu.make_async_remote_copy(src_ref=S3, dst_ref=R3.at[n], send_sem=cs.at[6 + n],
-                                            recv_sem=cr.at[6 + n], device_id=to, device_id_type=MESH)
+        cps = [pltpu.make_async_remote_copy(src_ref=S3, dst_ref=R3.at[n], send_sem=cs.at[10 + n],
+                                            recv_sem=cr.at[10 + n], device_id=to, device_id_type=MESH)
                for n, to in enumerate((py, pz, pyz))]
         for cp in cps:
             cp.start()
@@ -516,14 +544,12 @@
     sweep_pass(0, True, False)
     sweep_pass(1, False, False)
     residual_pass()
-    restrict_rows()
-    gather_chip()
     to_level1()
-    wide_exchange(L1, G1, RY1, SZ1, RZ1, 2)
+    wide_exchange(L1, G1, SY1, RY1, SZ1, RZ1, SD1, RD1, 4)
     first_two(L1, G1, V1)
     restrict_coarse(L1, L2, G1, V1, W1)
     restrict_lanes(L2, G2)
-    wide_exchange(L2, G2, RY2, SZ2, RZ2, 4)
+    wide_exchange(L2, G2, SY2, RY2, SZ2, RZ2, SD2, RD2, 7)
     first_two(L2, G2, V2)
     restrict_coarse(L2, L3, G2, V2, W2)
     gather_coarsest()
@@ -553,15 +579,14 @@
         vm = lambda *s: pltpu.VMEM(s, F32)
         scratch = [vm(130, PR, W), vm(130, PR, W), vm(N * PR, W), vm(N * PR, W), vm(N, N, W), vm(129, XR, W),
                    vm(XR, W), vm(XR, W), vm(5, 136, W), vm(GP * W, W), vm(2, N, W), vm(2, N, W), vm(2, N, W), vm(2, N, W)]
-        scratch += [vm(L2.rows, W)] * 3 + [vm(S * 48, W)] * 3
-        scratch += [vm(max(L2.rows, L3.rows), W), vm(33 * 40, W)]
+        scratch += [vm(L1.rows, W)] * 2 + [vm(L2.rows, W)] * 3 + [vm(S * 48, W)] * 3
         for L in (L1, L2):
-            z = up8((L.n + L.h) * (L.h + 1))
-            scratch += [vm((L.h + 1) * L.nk, W), vm(z, W), vm(z, W)]
+            z = up8((L.n + 1) * L.h)
+            scratch += [vm(L.h * (L.n + S), W)] * 2 + [vm(z, W)] * 2 + [vm(L.h * S, W)] * 2
         scratch += [vm(S * (L3.n + 1), W), vm(3, S * (L3.n + 1), W)]
         dma = pltpu.SemaphoreType.DMA
         scratch += [dma((2, NC)), dma((NC,)), dma((2,)), dma((2,)), dma((2, NC)), dma((2, NC)), dma((2, NC)), dma((2, NC)),
-                    dma((S + 1,)), dma((S + 1,))]
+                    dma((13,)), dma((13,))]
         return pl.pallas_call(
             functools.partial(body, h2),
             out_shape=jax.ShapeDtypeStruct(f.shape, F32),

time: 118 us -> 102 us (0.86)
  Pallas kernels: 110 us -> 94.2 us
    pallas_call x1, Pallas kernels: 110 us -> 94.2 us  [local(): pl.pallas_call(functools.partial(body, h2), out_shape=jax.ShapeDtypeStruc...]
where the time goes in v4:
time: 102 us
  Pallas kernels  94.2 us (92%)
  local copies, waits for them, and re-layouts  7.89 us (8%)
    pallas_call x1, Pallas kernels, local(): pl.pallas_call(functools.partial(body, h2), out_shape=jax.ShapeDtypeStruc...  94.2 us
    unnamed x1, local copies, waits for them, and re-layouts  7.89 us

profile of v4, /device:TPU:0, one launch (start us, length us, event | category | flops | bytes accessed | tf_op | source)
XLA Modules:
  0.0 102.1 jit_solution(12421181103848010823)
XLA Ops:
  0.0 94.2 %shard_map.28 = f32[128,128,128]{2,1,0:T(8,128)} custom-call(f32[128,128,128]{2,1,0:T(8,128)} %f_hbm.1, f32[128,128,128]{2,1,0:T(8,128)} %u_hbm.1), custom_call_target="tpu_custom_call" | custom-call | tf_op jit(solution)/shard_map/pallas_call | solution.py:590
  94.2 7.9 %copy.4 = f32[128,128,128]{2,1,0:T(8,128)} copy(f32[128,128,128]{2,1,0:T(8,128)} %shard_map.28) | data formatting | bytes 16777216

commit v5 on v4

--- a/solution.py
+++ b/solution.py
@@ -26,13 +26,14 @@
     def __init__(self, n, h, pj, kp, hb, ni, region, unroll, group):
         self.n, self.h, self.pj, self.kp, self.hb, self.ni = n, h, pj, kp, hb, ni
         self.region, self.unroll, self.group = region, unroll, group
+        self.size_own = 16
         self.nk = n + 2 * kp
         self.planes = n + 2 * pj
         self.rows = self.planes * self.nk
 
 
-L1 = Lev(64, 4, 6, 8, 8, 128, 68, 4, 1)
-L2 = Lev(32, 5, 10, 8, 8, 64, 40, 8, 12)
+L1 = Lev(64, 4, 6, 8, 8, 128, 68, 17, 1)
+L2 = Lev(32, 5, 10, 8, 8, 64, 40, 20, 12)
 L3 = Lev(16, 16, 18, 16, 16, 32, 32, 8, 10)
 EXTRA = 3
 
@@ -45,10 +46,10 @@
     return pl.ds(r, S)
 
 
-def body(h2, f_hbm, u_hbm, out_hbm, A, B, AT, BT, F, X, XP, RXP, TS, KS, PZ, RZ, PY, RY,
+def body(h2, f_hbm, u_hbm, B, A, AT, BT, F, X, XP, RXP, TS, KS, PZ, RZ, PY, RY,
          V1, W1, G2, V2, W2, G3, V3, W3,
          SY1, RY1, SZ1, RZ1, SD1, RD1, SY2, RY2, SZ2, RZ2, SD2, RD2, S3, R3,
-         ld, st, xs, xr, zs, zr, ys, yr, cs, cr):
+         ld, xs, xr, zs, zr, ys, yr, cs, cr):
     cx, cy, cz = lax.axis_index('sx'), lax.axis_index('sy'), lax.axis_index('sz')
     ninth = F32(1.0 / 9.0)
     px, py, pz = {'sx': 1 - cx}, {'sy': 1 - cy}, {'sz': 1 - cz}
@@ -74,9 +75,8 @@
         planes = pl.ds(k * CP, CP)
         src, dst = ((u_hbm, A.at[pl.ds(k * CP + 1, CP), pl.ds(S, W), :]), (f_hbm, F.at[planes]))[which]
         return pltpu.make_async_copy(src.at[planes], dst, ld.at[which, k])
-    for which in range(2):
-        for c in range(NC):
-            load(which, chunk_of(c)).start()
+    for c in range(NC):
+        load(0, chunk_of(c)).start()
 
     barrier = pltpu.get_barrier_semaphore()
     for p in (px, py, pz, pyz):
@@ -160,17 +160,21 @@
         def _():
             x_copy(par).start()
 
-    def stencil_pass(par, visit, dst, done):
+    def stencil_pass(par, visit, dst, done, arrive=None):
         src = flats[par]
         x_copy(par).wait()
         receive(par, chunk_of(0))
         side_sums(par, place(0))
+        if arrive is not None:
+            arrive(chunk_of(0))
 
         @pl.loop(0, NG)
         def _(g):
             @pl.when((g % GC == GC - 1) & (g < NG - 1))
             def _():
                 receive(par, chunk_of(g // GC + 1))
+                if arrive is not None:
+                    arrive(chunk_of(g // GC + 1))
             i0 = place(g)
             if dst is not None:
                 turn(dst, place((g + NG - 1) % NG), GP)
@@ -192,10 +196,6 @@
             done(NC - 1)
 
     def sweep_pass(par, first, last):
-        if first:
-            for k in range(NC):
-                load(1, k).wait()
-
         def visit(i, r, centre, total):
             fs = F[i, pl.ds(r, RB), :]
             if first:
@@ -205,21 +205,17 @@
 
         def done(c):
             k = chunk_of(c)
-            if last:
-                store(k).start()
-            else:
-                first_chunk(1 - par, c)
-                send(1 - par, k)
-        stencil_pass(par, visit, None if last else 1 - par, done)
-
-    def store(k):
-        return pltpu.make_async_copy(B.at[pl.ds(k * CP + 1, CP), pl.ds(S, W), :], out_hbm.at[pl.ds(k * CP, CP)], st.at[k])
+            first_chunk(1 - par, c)
+            send(1 - par, k)
+        stencil_pass(par, visit, None if last else 1 - par, None if last else done,
+                     (lambda k: load(1, k).wait()) if first else None)
 
     def start_level0():
         @pl.loop(0, NC)
         def _(c):
             k = chunk_of(c)
             load(0, k).wait()
+            load(1, k).start()
 
             @pl.loop(0, CP // S)
             def _(t):
@@ -331,29 +327,31 @@
         j0 = L.pj if own else L.pj - (L.region - L.n) * cy
         k0 = L.kp if own else L.kp - L.hb * cz
         count = L.n if own else L.n + L.hb
-        groups = (L.n if own else L.region) // L.unroll
+        planes = L.n if own else L.region
+        size = L.size_own if own else L.unroll
+        groups = planes // size
         lanes = lax.broadcasted_iota(jnp.int32, (count, W), 1)
 
         def place(g, p):
-            return pl.multiple_of((j0 + g * L.unroll + p) * L.nk + k0, S)
+            return pl.multiple_of((j0 + g * size + p) * L.nk + k0, S)
 
         def sides(g):
             out = []
-            for p in range(L.unroll):
+            for p in range(size):
                 c = src[pl.ds(place(g, p), count), :]
                 out.append(jnp.where(lanes == 0, 0.0, pltpu.roll(c, 1, 1)) + jnp.where(
                     lanes == L.ni - 1, 0.0, pltpu.roll(c, LAST, 1)))
             return out
 
         def keep(sums):
-            for p in range(L.unroll):
+            for p in range(size):
                 KS[pl.ds(p * count, count), :] = sums[p]
         keep(sides(0))
 
         @pl.loop(0, groups)
         def _(g):
             later = sides((g + 1) % groups)
-            for p in range(L.unroll):
+            for p in range(size):
                 r = place(g, p)
                 total = (src[pl.ds(r - L.nk, count), :] + src[pl.ds(r + L.nk, count), :]) + (
                     src[pl.ds(r - 1, count), :] + src[pl.ds(r + 1, count), :]) + KS[pl.ds(p * count, count), :]
@@ -566,8 +564,6 @@
     prolong_level0()
     sweep_pass(1, False, False)
     sweep_pass(0, False, True)
-    for k in range(NC):
-        store(k).wait()
 
 
 def solution(mesh):
@@ -577,24 +573,25 @@
         size = 2 * f.shape[1]
         h2 = 1.0 / float((size + 1) ** 2)
         vm = lambda *s: pltpu.VMEM(s, F32)
-        scratch = [vm(130, PR, W), vm(130, PR, W), vm(N * PR, W), vm(N * PR, W), vm(N, N, W), vm(129, XR, W),
-                   vm(XR, W), vm(XR, W), vm(5, 136, W), vm(GP * W, W), vm(2, N, W), vm(2, N, W), vm(2, N, W), vm(2, N, W)]
+        scratch = [vm(130, PR, W), vm(N * PR, W), vm(N * PR, W), vm(N, N, W), vm(129, XR, W),
+                   vm(XR, W), vm(XR, W), vm(5, 136, W), vm(17 * 72, W), vm(2, N, W), vm(2, N, W), vm(2, N, W), vm(2, N, W)]
         scratch += [vm(L1.rows, W)] * 2 + [vm(L2.rows, W)] * 3 + [vm(S * 48, W)] * 3
         for L in (L1, L2):
             z = up8((L.n + 1) * L.h)
             scratch += [vm(L.h * (L.n + S), W)] * 2 + [vm(z, W)] * 2 + [vm(L.h * S, W)] * 2
         scratch += [vm(S * (L3.n + 1), W), vm(3, S * (L3.n + 1), W)]
         dma = pltpu.SemaphoreType.DMA
-        scratch += [dma((2, NC)), dma((NC,)), dma((2,)), dma((2,)), dma((2, NC)), dma((2, NC)), dma((2, NC)), dma((2, NC)),
+        scratch += [dma((2, NC)), dma((2,)), dma((2,)), dma((2, NC)), dma((2, NC)), dma((2, NC)), dma((2, NC)),
                     dma((13,)), dma((13,))]
-        return pl.pallas_call(
+        out = pl.pallas_call(
             functools.partial(body, h2),
-            out_shape=jax.ShapeDtypeStruct(f.shape, F32),
+            out_shape=vm(130, PR, W),
             in_specs=[pl.BlockSpec(memory_space=pl.ANY)] * 2,
-            out_specs=pl.BlockSpec(memory_space=pl.ANY),
+            out_specs=pl.BlockSpec(memory_space=pltpu.VMEM),
             scratch_shapes=scratch,
-            compiler_params=pltpu.CompilerParams(collective_id=0, has_side_effects=True, vmem_limit_bytes=67043328),
+            compiler_params=pltpu.CompilerParams(collective_id=0, has_side_effects=True, vmem_limit_bytes=67043328 - 130 * PR * W * 4),
         )(f, u)
+        return out[1:N + 1, S:S + W]
 
     def run(rhs_grid, u_start):
         return jax.shard_map(local, mesh=mesh, in_specs=(spec, spec), out_specs=spec, check_vma=False)(rhs_grid, u_start)

time: 102 us -> 94.6 us (0.927)
  Pallas kernels: 94.2 us -> 90 us
  local copies, waits for them, and re-layouts: 7.89 us -> 4.45 us
    unnamed x1 -> x0, local copies, waits for them, and re-layouts: 7.89 us -> none
    slice x0 -> x1, local copies, waits for them, and re-layouts: none -> 4.45 us  [local(): return out[1:N + 1, S:S + W]]
    pallas_call x1, Pallas kernels: 94.2 us -> 90 us  [local(): pl.pallas_call(functools.partial(body, h2), out_shape=vm(130, PR, W), in_...]
where the time goes in v5:
time: 94.6 us; the launch traced here: 94.5 us
  Pallas kernels  90 us (95%)
  local copies, waits for them, and re-layouts  4.45 us (5%)
    pallas_call x1, Pallas kernels, local(): pl.pallas_call(functools.partial(body, h2), out_shape=vm(130, PR, W), in_...  90 us
    slice x1, local copies, waits for them, and re-layouts, local(): return out[1:N + 1, S:S + W]  4.45 us

profile of v5, /device:TPU:0, one launch (start us, length us, event | category | flops | bytes accessed | tf_op | source)
XLA Modules:
  0.0 94.5 jit_solution(15912094111570883251)
XLA Ops:
  0.0 90.0 %shard_map.28 = f32[130,144,128]{2,1,0:T(8,128)S(1)} custom-call(f32[128,128,128]{2,1,0:T(8,128)} %f_hbm.1, f32[128,128,128]{2,1,0:T(8,128)} %u_hbm.1), custom_call_target="tpu_custom_call" | custom-call | tf_op jit(solution)/shard_map/pallas_call | solution.py:586
  90.0 4.5 %slice.3 = f32[128,128,128]{2,1,0:T(8,128)} slice(f32[130,144,128]{2,1,0:T(8,128)S(1)} %shard_map.28), slice={[1:129], [8:136], [0:128]} | slice | bytes 16777216 | tf_op jit(solution)/shard_map/slice | solution.py:594

commit v6 on v5

--- a/solution.py
+++ b/solution.py
@@ -1,4 +1,5 @@
 import functools
+import math
 import jax
 import jax.numpy as jnp
 from jax import lax
@@ -46,7 +47,7 @@
     return pl.ds(r, S)
 
 
-def body(h2, f_hbm, u_hbm, B, A, AT, BT, F, X, XP, RXP, TS, KS, PZ, RZ, PY, RY,
+def body(h2, f_hbm, u_hbm, B, A, AT, F, BT, X, XP, RXP, TS, KS, PZ, RZ, PY, RY,
          V1, W1, G2, V2, W2, G3, V3, W3,
          SY1, RY1, SZ1, RZ1, SD1, RD1, SY2, RY2, SZ2, RZ2, SD2, RD2, S3, R3,
          ld, xs, xr, zs, zr, ys, yr, cs, cr):
@@ -160,7 +161,7 @@
         def _():
             x_copy(par).start()
 
-    def stencil_pass(par, visit, dst, done, arrive=None):
+    def stencil_pass(par, visit, dst, done, arrive=None, groups=NG):
         src = flats[par]
         x_copy(par).wait()
         receive(par, chunk_of(0))
@@ -168,9 +169,9 @@
         if arrive is not None:
             arrive(chunk_of(0))
 
-        @pl.loop(0, NG)
+        @pl.loop(0, groups)
         def _(g):
-            @pl.when((g % GC == GC - 1) & (g < NG - 1))
+            @pl.when((g % GC == GC - 1) & (g < groups - 1))
             def _():
                 receive(par, chunk_of(g // GC + 1))
                 if arrive is not None:
@@ -208,7 +209,7 @@
             first_chunk(1 - par, c)
             send(1 - par, k)
         stencil_pass(par, visit, None if last else 1 - par, None if last else done,
-                     (lambda k: load(1, k).wait()) if first else None)
+                     (lambda k: load(1, k).wait()) if first else None, NG // 2 if last else NG)
 
     def start_level0():
         @pl.loop(0, NC)
@@ -564,6 +565,52 @@
     prolong_level0()
     sweep_pass(1, False, False)
     sweep_pass(0, False, True)
+    for c in range(NC // 2, NC):
+        receive(0, chunk_of(c))
+
+
+def close(B, A, AT, F, out_hbm, O, KS, sems):
+    cx = lax.axis_index('sx')
+
+    def chunk_of(c):
+        return c * cx + (NC - 1 - c) * (1 - cx)
+
+    def place(g):
+        return chunk_of(g // GC) * CP + g % GC * GP
+
+    def rows(i, shift=0, count=W):
+        return pl.ds(i * PR + S + shift, count)
+
+    def store(c):
+        planes = pl.ds(chunk_of(c) * CP, CP)
+        src = B.at[pl.ds(chunk_of(c) * CP + 1, CP), pl.ds(S, W), :] if c < NC // 2 else O.at[pl.ds((c - NC // 2) * CP, CP)]
+        return pltpu.make_async_copy(src, out_hbm.at[planes], sems.at[c])
+    for c in range(NC // 2):
+        store(c).start()
+    src = A.reshape(A.shape[0] * PR, W)
+
+    def side_sums(i0):
+        for q in range(GP):
+            KS[pl.ds(q * W, W), :] = jnp.transpose(AT[rows(i0 + q, -1), :] + AT[rows(i0 + q, 1), :])
+    side_sums(place(NG // 2))
+    for c in range(NC // 2, NC):
+        @pl.loop(c * GC, (c + 1) * GC)
+        def _(g):
+            i0 = place(g)
+            for t in range(W // RB):
+                r = t * RB
+                um, uc = src[rows(i0, r, RB), :], src[rows(i0 + 1, r, RB), :]
+                for q in range(GP):
+                    un = src[rows(i0 + q + 2, r, RB), :]
+                    total = (um + un) + (src[rows(i0 + q + 1, r - 1, RB), :] + src[rows(i0 + q + 1, r + 1, RB), :]) + KS[
+                        pl.ds(q * W + r, RB), :]
+                    new = (3.0 * uc + (total + F[i0 + q, pl.ds(r, RB), :])) * F32(1 / 9)
+                    O[(g - NG // 2) * GP + q, pl.ds(r, RB), :] = new
+                    um, uc = uc, un
+            side_sums(place((g + 1) % NG))
+        store(c).start()
+    for c in range(NC):
+        store(c).wait()
 
 
 def solution(mesh):
@@ -573,7 +620,7 @@
         size = 2 * f.shape[1]
         h2 = 1.0 / float((size + 1) ** 2)
         vm = lambda *s: pltpu.VMEM(s, F32)
-        scratch = [vm(130, PR, W), vm(N * PR, W), vm(N * PR, W), vm(N, N, W), vm(129, XR, W),
+        scratch = [vm(N * PR, W), vm(129, XR, W),
                    vm(XR, W), vm(XR, W), vm(5, 136, W), vm(17 * 72, W), vm(2, N, W), vm(2, N, W), vm(2, N, W), vm(2, N, W)]
         scratch += [vm(L1.rows, W)] * 2 + [vm(L2.rows, W)] * 3 + [vm(S * 48, W)] * 3
         for L in (L1, L2):
@@ -583,15 +630,25 @@
         dma = pltpu.SemaphoreType.DMA
         scratch += [dma((2, NC)), dma((2,)), dma((2,)), dma((2, NC)), dma((2, NC)), dma((2, NC)), dma((2, NC)),
                     dma((13,)), dma((13,))]
-        out = pl.pallas_call(
+        resident = [vm(130, PR, W), vm(130, PR, W), vm(N * PR, W), vm(N, N, W)]
+        used = 4 * sum(math.prod(x.shape) for x in resident)
+        kept = pl.pallas_call(
             functools.partial(body, h2),
-            out_shape=vm(130, PR, W),
+            out_shape=resident,
             in_specs=[pl.BlockSpec(memory_space=pl.ANY)] * 2,
-            out_specs=pl.BlockSpec(memory_space=pltpu.VMEM),
+            out_specs=[pl.BlockSpec(memory_space=pltpu.VMEM)] * len(resident),
             scratch_shapes=scratch,
-            compiler_params=pltpu.CompilerParams(collective_id=0, has_side_effects=True, vmem_limit_bytes=67043328 - 130 * PR * W * 4),
+            compiler_params=pltpu.CompilerParams(collective_id=0, has_side_effects=True, vmem_limit_bytes=67043328 - used),
         )(f, u)
-        return out[1:N + 1, S:S + W]
+        kept = [pltpu.with_memory_space_constraint(x, pltpu.VMEM) for x in kept]
+        return pl.pallas_call(
+            close,
+            out_shape=jax.ShapeDtypeStruct(f.shape, F32),
+            in_specs=[pl.BlockSpec(memory_space=pltpu.VMEM)] * len(kept),
+            out_specs=pl.BlockSpec(memory_space=pl.ANY),
+            scratch_shapes=[vm(N // 2, N, W), vm(GP * W, W), dma((NC,))],
+            compiler_params=pltpu.CompilerParams(vmem_limit_bytes=67043328 - used),
+        )(*kept)
 
     def run(rhs_grid, u_start):
         return jax.shard_map(local, mesh=mesh, in_specs=(spec, spec), out_specs=spec, check_vma=False)(rhs_grid, u_start)

time: 94.6 us -> 92.2 us (0.975)
  local copies, waits for them, and re-layouts: 4.45 us -> 0 us
  Pallas kernels: 90 us -> 92.1 us
    slice x1 -> x0, local copies, waits for them, and re-layouts: 4.45 us -> none  [local(): return out[1:N + 1, S:S + W]]
    pallas_call x1 -> x2, Pallas kernels: 90 us -> 92.1 us  [the longest x1 88.7 us: local(): pl.pallas_call(functools.partial(body, h2), out_shape=resident, in_specs=...]
where the time goes in v6:
time: 92.2 us; the launch traced here: 92.1 us
  Pallas kernels  92.1 us (100%)
    pallas_call x1, Pallas kernels, local(): pl.pallas_call(functools.partial(body, h2), out_shape=resident, in_specs=...  88.7 us
    pallas_call x1, Pallas kernels, local(): pl.pallas_call(close, out_shape=jax.ShapeDtypeStruct(f.shape, F32), in_sp...  3.45 us

profile of v6, /device:TPU:0, one launch (start us, length us, event | category | flops | bytes accessed | tf_op | source)
XLA Modules:
  0.0 92.1 jit_solution(4936804037551882948)
XLA Ops:
  0.0 88.7 %shard_map.28 = (f32[130,144,128]{2,1,0:T(8,128)S(1)}, f32[130,144,128]{2,1,0:T(8,128)S(1)}, f32[18432,128]{1,0:T(8,128)S(1)}, f32[128,128,128]{2,1,0:T(8,128)S(1)}) custom-call(f32[128,128,128]{2,1,0:T(8,128)} %f_hbm.1, f32[128,128,128]{2,1,0:T(8,128)} %u_hbm.1), custom_call_target="tpu_custom_call" | custom-call | tf_op jit(solution)/shard_map/pallas_call | solution.py:635
  88.7 3.5 %shard_map.29 = f32[128,128,128]{2,1,0:T(8,128)} custom-call(f32[130,144,128]{2,1,0:T(8,128)S(1)} %get-tuple-element.9.B, f32[130,144,128]{2,1,0:T(8,128)S(1)} %get-tuple-element.10.A, f32[18432,128]{1,0:T(8,128)S(1)} %get-tuple-element.11.AT, f32[128,128,128]{2,1,0:T(8,128)S(1)} %get-tuple-element.12.F), custom_call_target="tpu_custom_call" | custom-call | tf_op jit(solution)/shard_map/pallas_call | solution.py:644

commit v7 on v6

--- a/solution.py
+++ b/solution.py
@@ -12,7 +12,7 @@
 NC = 4
 XR = 72
 CP = N // NC
-GP = 8
+GP = 16
 GC = CP // GP
 NG = N // GP
 RB = 32
@@ -144,12 +144,15 @@
         return chunk_of(g // GC) * CP + g % GC * GP
 
     def turn(par, i0, count):
+        base = pl.multiple_of(i0 * PR, S)
         for q in range(count):
-            turned[par][block(i0 + q), :] = jnp.transpose(flats[par][block(i0 + q + 1), :])
+            turned[par][pl.ds(base + (q * PR + S), W), :] = jnp.transpose(flats[par][pl.ds(base + ((q + 1) * PR + S), W), :])
 
     def side_sums(par, i0):
+        base = pl.multiple_of(i0 * PR, S)
         for q in range(GP):
-            KS[pl.ds(q * W, W), :] = jnp.transpose(turned[par][block(i0 + q, -1), :] + turned[par][block(i0 + q, 1), :])
+            lo, hi = (turned[par][pl.ds(base + (q * PR + S + d), W), :] for d in (-1, 1))
+            KS[pl.ds(q * W, W), :] = jnp.transpose(lo + hi)
 
     def after_chunk(g, done):
         @pl.when((g % GC == 0) & (g > 0))
@@ -179,14 +182,17 @@
             i0 = place(g)
             if dst is not None:
                 turn(dst, place((g + NG - 1) % NG), GP)
+            base = pl.multiple_of(i0 * PR, S)
+
+            def at(q, r):
+                return pl.ds(base + (q * PR + S + r), RB)
             for t in range(W // RB):
                 r = t * RB
-                um, uc = src[block(i0, r, RB), :], src[block(i0 + 1, r, RB), :]
+                um, uc = src[at(0, r), :], src[at(1, r), :]
                 for q in range(GP):
-                    un = src[block(i0 + q + 2, r, RB), :]
-                    total = (um + un) + (src[block(i0 + q + 1, r - 1, RB), :] + src[block(i0 + q + 1, r + 1, RB), :]) + KS[
-                        pl.ds(q * W + r, RB), :]
-                    visit(i0 + q, r, uc, total)
+                    un = src[at(q + 2, r), :]
+                    total = (um + un) + (src[at(q + 1, r - 1), :] + src[at(q + 1, r + 1), :]) + KS[pl.ds(q * W + r, RB), :]
+                    visit(i0, at, q, r, uc, total)
                     um, uc = uc, un
             side_sums(par, place((g + 1) % NG))
             if done is not None:
@@ -197,12 +203,12 @@
             done(NC - 1)
 
     def sweep_pass(par, first, last):
-        def visit(i, r, centre, total):
-            fs = F[i, pl.ds(r, RB), :]
+        def visit(i0, at, q, r, centre, total):
+            fs = F[i0 + q, pl.ds(r, RB), :]
             if first:
                 fs = fs * F32(h2)
-                F[i, pl.ds(r, RB), :] = fs
-            flats[1 - par][block(i + 1, r, RB), :] = (3.0 * centre + (total + fs)) * ninth
+                F[i0 + q, pl.ds(r, RB), :] = fs
+            flats[1 - par][at(q + 1, r), :] = (3.0 * centre + (total + fs)) * ninth
 
         def done(c):
             k = chunk_of(c)
@@ -225,53 +231,46 @@
             send(0, k)
 
     def residual_pass():
-        def visit(i, r, centre, total):
-            BT[block(i, r, RB), :] = F[i, pl.ds(r, RB), :] - 6.0 * centre + total
+        def visit(i0, at, q, r, centre, total):
+            BT[at(q, r), :] = F[i0 + q, pl.ds(r, RB), :] - 6.0 * centre + total
         stencil_pass(0, visit, None, None)
-        zero_turned(BT, (-1,))
-
-    def restrict_planes(i, weights, dst, dst_plane, jc, count):
-        acc = None
-        for di, w in weights:
-            base = (i + di) * PR + S + 2 * jc
-            lo, mid, hi = (BT[pl.ds(base + d, count, stride=2), :] for d in (-1, 0, 1))
-            tail = BT[pl.ds(base - 1, 1), :]
-            pair = (lo + hi) + 2.0 * mid if count > 1 else tail
-            pair = pair if w == 1 else pair * w
-            acc = pair if acc is None else acc + pair
-        dst[pl.ds(dst_plane * XR + jc, count), :] = acc
+        zero_turned(BT, (-1, W, W + 1))
 
     def restrict_rows(jc, count):
-        restrict_planes(0, ((0, 2.0), (1, 1)), X2, 64 * cx, jc, count)
-
-        @pl.loop(1, 64)
-        def _(i):
-            restrict_planes(2 * i, ((-1, 1), (0, 2.0), (1, 1)), X2, i + 64 * cx, jc, count)
-
-    JP = (24, 24, 16)
+        def line(plane):
+            lo, mid, hi = (BT[pl.ds(plane * PR + S + 2 * jc + d, count, stride=2), :] for d in (-1, 0, 1))
+            return (lo + hi) + 2.0 * mid
+
+        def put(i, value):
+            X2[pl.ds((i + 64 * cx) * XR + jc, count), :] = value
+
+        def step(t, last):
+            for q in range(3):
+                i = 1 + t * 3 + q
+                odd = line(2 * i + 1)
+                put(i, (last + odd) + 2.0 * line(2 * i))
+                last = odd
+            return last
+        odd = line(1)
+        put(0, odd + 2.0 * line(0))
+        XP[pl.ds(jc, count), :] = lax.fori_loop(0, 21, step, odd)
+
+    JP = (24, 24, 17)
 
     def to_level1():
-        spans = []
+        own = pl.ds(64 * cx, 64)
+        copies = []
         for m, count in enumerate(JP):
-            jc = sum(JP[:m])
-            pieces = ((jc, count),) if m < 2 else ((jc, count), (jc + count, 1))
-            spans.append((jc, pieces))
-        for jc, pieces in spans:
-            for piece in pieces:
-                restrict_planes(LAST, ((0, 1),), XP, 0, *piece)
-        own = pl.ds(64 * cx, 64)
-        whole = [pltpu.make_async_remote_copy(src_ref=XP, dst_ref=RXP, send_sem=cs.at[3], recv_sem=cr.at[3],
-                                              device_id=px, device_id_type=MESH)]
-        whole[0].start()
-        for m, (jc, pieces) in enumerate(spans):
-            for piece in pieces:
-                restrict_rows(*piece)
-            part = X.at[own, pl.ds(jc, JP[0]), :]
-            whole.append(pltpu.make_async_remote_copy(src_ref=part, dst_ref=part, send_sem=cs.at[m], recv_sem=cr.at[m],
-                                                      device_id=px, device_id_type=MESH))
-            whole[-1].start()
+            jc = m * JP[0]
+            restrict_rows(jc, count)
+            part, rows = X.at[own, pl.ds(jc, JP[0]), :], pl.ds(jc, JP[0])
+            pair = [pltpu.make_async_remote_copy(src_ref=src, dst_ref=dst, send_sem=cs.at[2 * m + n], recv_sem=cr.at[2 * m + n],
+                                                 device_id=px, device_id_type=MESH)
+                    for n, (src, dst) in enumerate(((XP.at[rows, :], RXP.at[rows, :]), (part, part)))]
+            for cp in pair:
+                cp.start()
+            copies.append(pair)
         zero_rows(AT, L1.rows)
-        whole[0].wait()
 
         def tile(jc, q):
             TS[q, pl.ds(S, W), :] = jnp.transpose(X2[pl.ds(jc, W, stride=XR), :])
@@ -280,8 +279,10 @@
             G1[pl.ds(pl.multiple_of(base, S), 64), :] = ((lo + hi) + 2.0 * mid) * F32(1 / 16)
             G1[pl.ds(base + 64, 1), :] = TS[q, pl.ds(135, 1), :] * F32(1 / 16)
 
-        for m, (jc, pieces) in enumerate(spans):
-            whole[m + 1].wait()
+        for m, pair in enumerate(copies):
+            for cp in pair:
+                cp.wait()
+            jc = m * JP[0]
             rows = pl.ds(jc, JP[0])
             X2[pl.ds(64 * XR + jc, JP[0]), :] += jnp.where(cx == 0, XP[rows, :], RXP[rows, :])
 
@@ -333,13 +334,14 @@
         groups = planes // size
         lanes = lax.broadcasted_iota(jnp.int32, (count, W), 1)
 
-        def place(g, p):
-            return pl.multiple_of((j0 + g * size + p) * L.nk + k0, S)
+        def place(g):
+            return pl.multiple_of((j0 + g * size) * L.nk + k0, S)
 
         def sides(g):
             out = []
+            base = place(g)
             for p in range(size):
-                c = src[pl.ds(place(g, p), count), :]
+                c = src[pl.ds(base + p * L.nk, count), :]
                 out.append(jnp.where(lanes == 0, 0.0, pltpu.roll(c, 1, 1)) + jnp.where(
                     lanes == L.ni - 1, 0.0, pltpu.roll(c, LAST, 1)))
             return out
@@ -352,11 +354,10 @@
         @pl.loop(0, groups)
         def _(g):
             later = sides((g + 1) % groups)
+            base = place(g)
             for p in range(size):
-                r = place(g, p)
-                total = (src[pl.ds(r - L.nk, count), :] + src[pl.ds(r + L.nk, count), :]) + (
-                    src[pl.ds(r - 1, count), :] + src[pl.ds(r + 1, count), :]) + KS[pl.ds(p * count, count), :]
-                visit(pl.ds(r, count), src[pl.ds(r, count), :], total)
+                lo, hi, below, above, c = (src[pl.ds(base + (p * L.nk + d), count), :] for d in (-L.nk, L.nk, -1, 1, 0))
+                visit(pl.ds(base + p * L.nk, count), c, (lo + hi) + (below + above) + KS[pl.ds(p * count, count), :])
             keep(later)
 
     def first_two(L, G, V):
@@ -427,8 +428,8 @@
             x = parts[0][p * hr:p * hr + cells] + parts[1][p * hr:p * hr + cells]
             x = x + parts[2][:cells] if p == 0 else x
             S3[pl.ds(p * cells, cells), :] = x * F32(1 / 16)
-        cps = [pltpu.make_async_remote_copy(src_ref=S3, dst_ref=R3.at[n], send_sem=cs.at[10 + n],
-                                            recv_sem=cr.at[10 + n], device_id=to, device_id_type=MESH)
+        cps = [pltpu.make_async_remote_copy(src_ref=S3, dst_ref=R3.at[n], send_sem=cs.at[12 + n],
+                                            recv_sem=cr.at[12 + n], device_id=to, device_id_type=MESH)
                for n, to in enumerate((py, pz, pyz))]
         for cp in cps:
             cp.start()
@@ -544,11 +545,11 @@
     sweep_pass(1, False, False)
     residual_pass()
     to_level1()
-    wide_exchange(L1, G1, SY1, RY1, SZ1, RZ1, SD1, RD1, 4)
+    wide_exchange(L1, G1, SY1, RY1, SZ1, RZ1, SD1, RD1, 6)
     first_two(L1, G1, V1)
     restrict_coarse(L1, L2, G1, V1, W1)
     restrict_lanes(L2, G2)
-    wide_exchange(L2, G2, SY2, RY2, SZ2, RZ2, SD2, RD2, 7)
+    wide_exchange(L2, G2, SY2, RY2, SZ2, RZ2, SD2, RD2, 9)
     first_two(L2, G2, V2)
     restrict_coarse(L2, L3, G2, V2, W2)
     gather_coarsest()
@@ -597,13 +598,16 @@
         @pl.loop(c * GC, (c + 1) * GC)
         def _(g):
             i0 = place(g)
+            base = pl.multiple_of(i0 * PR, S)
+
+            def at(q, r):
+                return pl.ds(base + (q * PR + S + r), RB)
             for t in range(W // RB):
                 r = t * RB
-                um, uc = src[rows(i0, r, RB), :], src[rows(i0 + 1, r, RB), :]
+                um, uc = src[at(0, r), :], src[at(1, r), :]
                 for q in range(GP):
-                    un = src[rows(i0 + q + 2, r, RB), :]
-                    total = (um + un) + (src[rows(i0 + q + 1, r - 1, RB), :] + src[rows(i0 + q + 1, r + 1, RB), :]) + KS[
-                        pl.ds(q * W + r, RB), :]
+                    un = src[at(q + 2, r), :]
+                    total = (um + un) + (src[at(q + 1, r - 1), :] + src[at(q + 1, r + 1), :]) + KS[pl.ds(q * W + r, RB), :]
                     new = (3.0 * uc + (total + F[i0 + q, pl.ds(r, RB), :])) * F32(1 / 9)
                     O[(g - NG // 2) * GP + q, pl.ds(r, RB), :] = new
                     um, uc = uc, un
@@ -621,7 +625,7 @@
         h2 = 1.0 / float((size + 1) ** 2)
         vm = lambda *s: pltpu.VMEM(s, F32)
         scratch = [vm(N * PR, W), vm(129, XR, W),
-                   vm(XR, W), vm(XR, W), vm(5, 136, W), vm(17 * 72, W), vm(2, N, W), vm(2, N, W), vm(2, N, W), vm(2, N, W)]
+                   vm(XR, W), vm(XR, W), vm(5, 136, W), vm(GP * W, W), vm(2, N, W), vm(2, N, W), vm(2, N, W), vm(2, N, W)]
         scratch += [vm(L1.rows, W)] * 2 + [vm(L2.rows, W)] * 3 + [vm(S * 48, W)] * 3
         for L in (L1, L2):
             z = up8((L.n + 1) * L.h)
@@ -629,7 +633,7 @@
         scratch += [vm(S * (L3.n + 1), W), vm(3, S * (L3.n + 1), W)]
         dma = pltpu.SemaphoreType.DMA
         scratch += [dma((2, NC)), dma((2,)), dma((2,)), dma((2, NC)), dma((2, NC)), dma((2, NC)), dma((2, NC)),
-                    dma((13,)), dma((13,))]
+                    dma((15,)), dma((15,))]
         resident = [vm(130, PR, W), vm(130, PR, W), vm(N * PR, W), vm(N, N, W)]
         used = 4 * sum(math.prod(x.shape) for x in resident)
         kept = pl.pallas_call(

time: 92.2 us -> 89.7 us (0.973)
  Pallas kernels: 92.1 us -> 89.6 us
    pallas_call x1, Pallas kernels: 88.7 us -> 86.2 us  [local(): pl.pallas_call(functools.partial(body, h2), out_shape=resident, in_specs=...]
where the time goes in v7:
time: 89.7 us; the launch traced here: 89.6 us
  Pallas kernels  89.6 us (100%)
    pallas_call x1, Pallas kernels, local(): pl.pallas_call(functools.partial(body, h2), out_shape=resident, in_specs=...  86.2 us
    pallas_call x1, Pallas kernels, local(): pl.pallas_call(close, out_shape=jax.ShapeDtypeStruct(f.shape, F32), in_sp...  3.4 us

profile of v7, /device:TPU:0, one launch (start us, length us, event | category | flops | bytes accessed | tf_op | source)
XLA Modules:
  0.0 89.6 jit_solution(9811238215719429003)
XLA Ops:
  0.0 86.2 %shard_map.28 = (f32[130,144,128]{2,1,0:T(8,128)S(1)}, f32[130,144,128]{2,1,0:T(8,128)S(1)}, f32[18432,128]{1,0:T(8,128)S(1)}, f32[128,128,128]{2,1,0:T(8,128)S(1)}) custom-call(f32[128,128,128]{2,1,0:T(8,128)} %f_hbm.1, f32[128,128,128]{2,1,0:T(8,128)} %u_hbm.1), custom_call_target="tpu_custom_call" | custom-call | tf_op jit(solution)/shard_map/pallas_call | solution.py:639
  86.2 3.4 %shard_map.29 = f32[128,128,128]{2,1,0:T(8,128)} custom-call(f32[130,144,128]{2,1,0:T(8,128)S(1)} %get-tuple-element.9.B, f32[130,144,128]{2,1,0:T(8,128)S(1)} %get-tuple-element.10.A, f32[18432,128]{1,0:T(8,128)S(1)} %get-tuple-element.11.AT, f32[128,128,128]{2,1,0:T(8,128)S(1)} %get-tuple-element.12.F), custom_call_target="tpu_custom_call" | custom-call | tf_op jit(solution)/shard_map/pallas_call | solution.py:648
